TPU v7x, 128 devices: a whole 4x4x4 slice. The times are simulated.
128 devices in a mesh: dp: 8 (over z, y_lo), tensor: 16 (over x, y_hi, core).
Axes of the slice: x: 4, y: 4 (y_hi: 2, y_lo: 2; y = y_hi * 2 + y_lo), z: 4, core: 2. Of those that a mesh axis runs over, the one named last changes fastest.
Arguments:
- tokens: bfloat16 [2048, 4096], P(('dp', 'tensor')), may hold values from -4 to 4
- lengths: int32 [8], replicated, may hold values from 64 to 256, as said below
- norm_gains: float32 [2, 4096], replicated, may hold values from 0.25 to 1.75
- query_weight: bfloat16 [2, 4096, 4096], P(None, None, 'tensor'), may hold values from -0.09375 to 0.09375
- key_weight: bfloat16 [2, 4096, 1024], P(None, None, 'tensor'), may hold values from -0.09375 to 0.09375
- value_weight: bfloat16 [2, 4096, 1024], P(None, None, 'tensor'), may hold values from -0.09375 to 0.09375
- out_weight: bfloat16 [2, 4096, 4096], P(None, 'tensor'), may hold values from -0.09375 to 0.09375
- query_probe: bfloat16 [2, 4096, 4096], P(None, 'dp', 'tensor'), may hold values from -0.09375 to 0.09375
- key_probe: bfloat16 [2, 4096, 1024], P(None, 'dp', 'tensor'), may hold values from -0.09375 to 0.09375
- value_probe: bfloat16 [2, 4096, 1024], P(None, 'dp', 'tensor'), may hold values from -0.09375 to 0.09375
- out_probe: bfloat16 [2, 4096, 4096], P(None, 'tensor', 'dp'), may hold values from -0.09375 to 0.09375
Outputs:
- query_product: float32 [2, 4096, 4096], P(None, 'dp', 'tensor')
- key_product: float32 [2, 4096, 1024], P(None, 'dp', 'tensor')
- value_product: float32 [2, 4096, 1024], P(None, 'dp', 'tensor')
- out_product: float32 [2, 4096, 4096], P(None, 'tensor', 'dp')
Inputs may be any that keep to these rules, and one draw needn't show every extreme that they name: lengths[i] counts the leading valid positions of sequence i; the last sequence is full.
All inputs are finite; a program needn't handle non-finite values.
Results may differ from a plain program's by a relative error of at most 0.035.
Values may be sent and summed in bfloat16 or wider, within the bound.
No kernel may reach another device: no remote copies, remote signals or barrier semaphores. Data moves between devices by JAX's collectives and lax.ppermute only.
A program may use at most 128 MiB of HBM per device.

v0:
```python
import math

import jax
import jax.numpy as jnp
from jax import lax
from jax.sharding import PartitionSpec as P

HD = 128
LEN = 256


EPS = 1e-05
THETA = 500000.0


def turned_gather(arrays, axis, dims):
    turned = [jnp.moveaxis(a, dim, 0) for a, dim in zip(arrays, dims)]
    both = jnp.concatenate([t.reshape(len(t), -1) for t in turned], axis=1)
    result, at, done = (lax.all_gather(both, axis, axis=0, tiled=True), 0, [])
    for t, dim in zip(turned, dims):
        share = result[:, at : at + t[0].size].reshape(-1, *t.shape[1:])
        done.append(jnp.moveaxis(share, 0, dim))
        at += t[0].size
    return tuple(done)


def sent_together(arrays, axis, dim, along):
    widths = [a.shape[along] for a in arrays]
    both = jnp.concatenate(arrays, axis=along)
    result = lax.all_gather(both, axis, axis=dim, tiled=True)
    return tuple(jnp.split(result, [sum(widths[:k]) for k in range(1, len(widths))], axis=along))


def swapped(value, axis, apart):
    mask = 2**apart
    pairs = [(source, source ^ mask) for source in range(lax.axis_size(axis))]
    return lax.ppermute(value, axis, pairs)


def split_up(x, dim, length):
    before, after = (x.shape[:dim], x.shape[dim + 1 :])
    return jnp.moveaxis(x.reshape(*before, length, -1, *after), dim, 0)


def sum_at_owner(x, axis, dim):
    pieces = split_up(x, dim, lax.axis_size(axis))
    arrived = lax.all_to_all(pieces, axis, split_axis=0, concat_axis=0, tiled=True)
    return arrived.astype(jnp.float32).sum(axis=0)


def side_by_side(arrays, axis, dim, along):
    ends, at = ([], 0)
    for a in arrays[:-1]:
        at += a.shape[along]
        ends.append(at)
    both = jnp.concatenate(arrays, axis=along)
    return tuple(
        jnp.split(lax.psum_scatter(both, axis, scatter_dimension=dim, tiled=True), ends, axis=along)
    )


def sum_packed(arrays, axis, dims):
    length = lax.axis_size(axis)
    pieces = [split_up(a, dim, length) for a, dim in zip(arrays, dims)]
    lines = jnp.concatenate([b.reshape(length, -1) for b in pieces], axis=1)
    width = max(16, -(-lines.shape[1] // 1024) * 8)
    lines = jnp.pad(lines, ((0, 0), (0, width * 128 - lines.shape[1]))).reshape(-1, 128)
    ravelled, at, done = (lax.psum_scatter(lines, axis, tiled=True).reshape(-1), 0, [])
    for b in pieces:
        part = b[0]
        done.append(ravelled[at : at + part.size].reshape(part.shape))
        at += part.size
    return tuple(done)


def multiply(pattern, left_side, right_side):
    return jnp.einsum(pattern, left_side, right_side, preferred_element_type=jnp.float32)


def matmul(left_side, right_side):
    return jnp.dot(left_side, right_side, preferred_element_type=jnp.float32)


def contract_rows(left_side, right_side):
    return lax.dot_general(
        left_side, right_side, (((0,), (0,)), ((), ())), preferred_element_type=jnp.float32
    )


def contract_last(left_side, right_side):
    return lax.dot_general(
        left_side, right_side, (((1,), (1,)), ((), ())), preferred_element_type=jnp.float32
    )


def rope_tables(length, head_size):
    position = jnp.arange(length).astype(jnp.float32)
    column = jnp.arange(head_size // 2).astype(jnp.float32)
    frequency = jnp.exp(-math.log(THETA) * 2.0 * column / head_size)
    angles = position[:, None] * frequency[None, :]
    return (jnp.cos(angles), jnp.sin(angles))


def rotate(values, cosine_table, sine_table, direction):
    middle = values.shape[-1] // 2
    leading = values[..., :middle]
    trailing = values[..., middle:]
    cosine = cosine_table[None, :, None, :]
    sine_part = direction * sine_table[None, :, None, :]
    return jnp.concatenate(
        [leading * cosine - trailing * sine_part, trailing * cosine + leading * sine_part], axis=-1
    )


def allowed_mask(size, length):
    row_index = jnp.arange(size)[:, None]
    column_index = jnp.arange(size)[None, :]
    return (column_index <= row_index) & (column_index < length)


def attend(queries, key_heads, value_heads, tangent_queries, tangent_keys, tangent_values, length):
    repeat = queries.shape[1] // key_heads.shape[1]
    key_heads = jnp.repeat(key_heads, repeat, axis=1)
    value_heads = jnp.repeat(value_heads, repeat, axis=1)
    tangent_keys = jnp.repeat(tangent_keys, repeat, axis=1)
    tangent_values = jnp.repeat(tangent_values, repeat, axis=1)
    scaling = 1.0 / math.sqrt(queries.shape[-1])
    allowed = allowed_mask(queries.shape[0], length)[None]
    scores = multiply("ihd,jhd->hij", queries, key_heads) * scaling
    powers = jnp.where(allowed, jnp.exp(scores), 0.0)
    weights = powers / jnp.sum(powers, axis=-1, keepdims=True)
    weights_low = weights.astype(jnp.bfloat16)
    blended = multiply("hij,jhd->ihd", weights_low, value_heads).astype(jnp.bfloat16)
    tangent_scores = (
        multiply("ihd,jhd->hij", tangent_queries, key_heads)
        + multiply("ihd,jhd->hij", queries, tangent_keys)
    ) * scaling
    tangent_weights = weights * (
        tangent_scores - jnp.sum(weights * tangent_scores, axis=-1, keepdims=True)
    )
    tangent_blended = multiply(
        "hij,jhd->ihd", tangent_weights.astype(jnp.bfloat16), value_heads
    ) + multiply("hij,jhd->ihd", weights_low, tangent_values)
    return (blended, tangent_blended.astype(jnp.bfloat16))


def attend_back(queries, key_heads, value_heads, grad_mixed, length):
    repeat = queries.shape[1] // key_heads.shape[1]
    key_heads = jnp.repeat(key_heads, repeat, axis=1)
    value_heads = jnp.repeat(value_heads, repeat, axis=1)
    scaling = 1.0 / math.sqrt(queries.shape[-1])
    allowed = allowed_mask(queries.shape[0], length)[None]
    scores = multiply("ihd,jhd->hij", queries, key_heads) * scaling
    powers = jnp.where(allowed, jnp.exp(scores), 0.0)
    weights = powers / jnp.sum(powers, axis=-1, keepdims=True)
    weights_low = weights.astype(jnp.bfloat16)
    grad_weights = multiply("ihd,jhd->hij", grad_mixed, value_heads)
    grad_values = multiply("hij,ihd->jhd", weights_low, grad_mixed)
    grad_scores = (
        weights * (grad_weights - jnp.sum(weights * grad_weights, axis=-1, keepdims=True)) * scaling
    ).astype(jnp.bfloat16)
    grad_queries = multiply("hij,jhd->ihd", grad_scores, key_heads)
    grad_keys = multiply("hij,ihd->jhd", grad_scores, queries)
    return (grad_queries, grad_keys, grad_values)


def normalize(stream, gain_row):
    wide_stream = stream.astype(jnp.float32)
    inverse = lax.rsqrt(jnp.mean(wide_stream * wide_stream, axis=-1, keepdims=True) + EPS)
    return (wide_stream, inverse, (wide_stream * inverse * gain_row).astype(jnp.bfloat16))


def norm_tangent(wide_stream, inverse, tangent, gain_row):
    shift = jnp.mean(wide_stream * tangent, axis=-1, keepdims=True)
    return (
        gain_row * (tangent * inverse - wide_stream * inverse * inverse * inverse * shift)
    ).astype(jnp.bfloat16)


def norm_back(wide_stream, inverse, grad_normed, gain_row):
    scaled = grad_normed * gain_row
    shift = jnp.mean(wide_stream * scaled, axis=-1, keepdims=True)
    return inverse * (scaled - wide_stream * inverse * inverse * shift)


def body(
    tokens,
    lengths,
    norm_gains,
    query_weight,
    key_weight,
    value_weight,
    out_weight,
    query_probe,
    key_probe,
    value_probe,
    out_probe,
):
    tensor_count = lax.axis_size("tensor")
    tensor_index = lax.axis_index("tensor")
    data_index = lax.axis_index("dp")
    share_rows = tokens.shape[0]
    group_rows = share_rows * tensor_count
    seq_count = group_rows // LEN
    layer_count = query_weight.shape[0]
    half_width = key_weight.shape[2]
    cosine_table, sine_table = rope_tables(LEN, HD)
    group_lengths = lax.dynamic_slice_in_dim(lengths, data_index * seq_count, seq_count)
    position = jnp.arange(group_rows) % LEN
    group_mask = (position < jnp.repeat(group_lengths, LEN)).astype(jnp.float32)
    share_mask = lax.dynamic_slice_in_dim(group_mask, tensor_index * share_rows, share_rows)
    lower_half = tensor_index % 2 == 0

    def heads_of(values):
        return values.reshape(seq_count, LEN, -1, HD)

    def join_halves(own_part, other_part):
        return jnp.where(
            lower_half,
            jnp.concatenate([own_part, other_part], axis=-1),
            jnp.concatenate([other_part, own_part], axis=-1),
        )

    def own_columns(values):
        return jnp.where(lower_half, values[:, :half_width], values[:, half_width:])

    def other_columns(values):
        return jnp.where(lower_half, values[:, half_width:], values[:, :half_width])

    query_full_probe, key_own_probe, value_own_probe, out_full_probe = turned_gather(
        (query_probe, key_probe, value_probe, out_probe), "dp", (1, 1, 1, 2)
    )
    owned_parts = (key_weight, value_weight, key_own_probe, value_own_probe)
    key_full, value_full, key_full_probe, value_full_probe = owned_parts
    stream = tokens
    tangent = None
    stored = []
    for layer_index in range(layer_count):
        final_layer = layer_index == layer_count - 1
        gain_row = norm_gains[layer_index]
        wide_stream, inverse, normed = normalize(stream, gain_row)
        tangent_normed = (
            None if tangent is None else norm_tangent(wide_stream, inverse, tangent, gain_row)
        )
        if tangent_normed is None:
            normed_all = lax.all_gather(normed, "tensor", axis=0, tiled=True)
            tangent_all = None
        else:
            normed_all, tangent_all = sent_together((normed, tangent_normed), "tensor", 0, 1)

        def project(weight, probe_part):
            primal = matmul(normed_all, weight)
            moved_part = matmul(normed_all, probe_part)
            if tangent_all is not None:
                moved_part = moved_part + matmul(tangent_all, weight)
            return (primal, moved_part)

        query_primal, query_moved = project(
            query_weight[layer_index], query_full_probe[layer_index]
        )
        key_primal, key_moved = project(key_full[layer_index], key_full_probe[layer_index])
        value_primal, value_moved = project(value_full[layer_index], value_full_probe[layer_index])
        own_projections = (key_primal, key_moved, value_primal, value_moved)
        other_projections = (
            swapped(own_projections[0].astype(jnp.bfloat16), "tensor", 0).astype(jnp.float32),
            swapped(own_projections[1].astype(jnp.bfloat16), "tensor", 0).astype(jnp.float32),
            swapped(own_projections[2].astype(jnp.bfloat16), "tensor", 0).astype(jnp.float32),
            swapped(own_projections[3].astype(jnp.bfloat16), "tensor", 0).astype(jnp.float32),
        )
        key_primal, key_moved, value_primal, value_moved = [
            join_halves(own_part, other_part)
            for own_part, other_part in zip(own_projections, other_projections)
        ]
        queries = rotate(heads_of(query_primal), cosine_table, sine_table, 1.0).astype(jnp.bfloat16)
        key_heads = rotate(heads_of(key_primal), cosine_table, sine_table, 1.0).astype(jnp.bfloat16)
        value_heads = heads_of(value_primal).astype(jnp.bfloat16)
        tangent_queries = rotate(heads_of(query_moved), cosine_table, sine_table, 1.0).astype(
            jnp.bfloat16
        )
        tangent_keys = rotate(heads_of(key_moved), cosine_table, sine_table, 1.0).astype(
            jnp.bfloat16
        )
        tangent_values = heads_of(value_moved).astype(jnp.bfloat16)
        blended, tangent_blended = lax.map(
            lambda pieces: attend(*pieces),
            (
                queries,
                key_heads,
                value_heads,
                tangent_queries,
                tangent_keys,
                tangent_values,
                group_lengths,
            ),
        )
        blended = blended.reshape(group_rows, -1)
        tangent_blended = tangent_blended.reshape(group_rows, -1)
        tangent_part = matmul(tangent_blended, out_weight[layer_index]) + matmul(
            blended, out_full_probe[layer_index]
        )
        if final_layer:
            tangent_sum = sum_at_owner(tangent_part.astype(jnp.bfloat16), "tensor", 0)
        else:
            primal_part = matmul(blended, out_weight[layer_index])
            primal_sum, tangent_sum = tuple(
                (
                    part.astype(jnp.float32)
                    for part in side_by_side(
                        (primal_part.astype(jnp.bfloat16), tangent_part.astype(jnp.bfloat16)),
                        "tensor",
                        0,
                        1,
                    )
                )
            )
        stored.append((wide_stream, inverse, normed_all, queries, key_heads, value_heads, blended))
        if not final_layer:
            stream = (wide_stream + primal_sum).astype(jnp.bfloat16)
        tangent = tangent_sum if tangent is None else tangent + tangent_sum
    cotangent = share_mask[:, None] * tangent
    collected = [None] * layer_count
    for layer_index in reversed(range(layer_count)):
        wide_stream, inverse, normed_all, queries, key_heads, value_heads, blended = stored[
            layer_index
        ]
        cotangent_low = cotangent.astype(jnp.bfloat16)
        cotangent_low = lax.all_gather(cotangent_low, "tensor", axis=0, tiled=True)
        out_product = contract_rows(blended, cotangent_low)
        grad_mixed = contract_last(cotangent_low, out_weight[layer_index]).astype(jnp.bfloat16)
        grad_queries, grad_keys, grad_values = lax.map(
            lambda pieces: attend_back(*pieces),
            (queries, key_heads, value_heads, heads_of(grad_mixed), group_lengths),
        )
        key_count = key_heads.shape[2]
        query_low = (
            rotate(grad_queries, cosine_table, sine_table, -1.0)
            .astype(jnp.bfloat16)
            .reshape(group_rows, -1)
        )
        key_grouped = grad_keys.reshape(seq_count, LEN, key_count, -1, HD).sum(axis=3)
        key_low = (
            rotate(key_grouped, cosine_table, sine_table, -1.0)
            .astype(jnp.bfloat16)
            .reshape(group_rows, -1)
        )
        value_low = (
            grad_values.reshape(seq_count, LEN, key_count, -1, HD)
            .sum(axis=3)
            .astype(jnp.bfloat16)
            .reshape(group_rows, -1)
        )
        query_product = contract_rows(normed_all, query_low)
        key_mine = own_columns(key_low)
        value_mine = own_columns(value_low)
        key_recv, value_recv = swapped(
            (other_columns(key_low), other_columns(value_low)), "tensor", 0
        )
        key_product = contract_rows(normed_all, key_mine) + contract_rows(normed_all, key_recv)
        value_product = contract_rows(normed_all, value_mine) + contract_rows(
            normed_all, value_recv
        )
        collected[layer_index] = tuple(
            (
                part.astype(jnp.float32)
                for part in sum_packed(
                    (
                        query_product.astype(jnp.bfloat16),
                        key_product.astype(jnp.bfloat16),
                        value_product.astype(jnp.bfloat16),
                        out_product.astype(jnp.bfloat16),
                    ),
                    "dp",
                    (0, 0, 0, 1),
                )
            )
        )
        if layer_index > 0:
            grad_part = contract_last(query_low, query_weight[layer_index])
            key_own_weight = key_full[layer_index]
            value_own_weight = value_full[layer_index]
            grad_part = (
                grad_part
                + contract_last(key_mine, key_own_weight)
                + contract_last(key_recv, key_own_weight)
            )
            grad_part = (
                grad_part
                + contract_last(value_mine, value_own_weight)
                + contract_last(value_recv, value_own_weight)
            )
            grad_normed = sum_at_owner(grad_part.astype(jnp.bfloat16), "tensor", 0)
            cotangent = cotangent + norm_back(
                wide_stream, inverse, grad_normed, norm_gains[layer_index]
            )
    query_stack = jnp.stack([collected[number][0] for number in range(layer_count)])
    key_stack = jnp.stack([collected[number][1] for number in range(layer_count)])
    value_stack = jnp.stack([collected[number][2] for number in range(layer_count)])
    out_stack = jnp.stack([collected[number][3] for number in range(layer_count)])
    return (query_stack, key_stack, value_stack, out_stack)


def solution(mesh):
    placed = (
        P(("dp", "tensor"), None),
        P(),
        P(),
        P(None, None, "tensor"),
        P(None, None, "tensor"),
        P(None, None, "tensor"),
        P(None, "tensor", None),
        P(None, "dp", "tensor"),
        P(None, "dp", "tensor"),
        P(None, "dp", "tensor"),
        P(None, "tensor", "dp"),
    )
    return jax.shard_map(
        body,
        mesh=mesh,
        in_specs=placed,
        out_specs=(
            P(None, "dp", "tensor"),
            P(None, "dp", "tensor"),
            P(None, "dp", "tensor"),
            P(None, "tensor", "dp"),
        ),
        check_vma=False,
    )
```

profile of v0, /device:TPU:1, one launch (start us, length us, event | category | flops | bytes accessed | tf_op | source)
XLA Modules:
  0.0 920.6 jit_solution(7696534953255749129)
XLA Ops:
  14.5 3.8 slice_bitcast_fusion.7
  18.3 3.0 copy.49
  24.2 38.5 %all-gather.6.cloned.1.call-done = bf16[256,4096]{1,0:T(8,128)(2,1)} async-done(((bf16[16,4096]{1,0:T(8,128)(2,1)}), bf16[256,4096]{1,0:T(8,128)(2,1)}) %all-gather.6.cloned.1.call-update) | async-done | bytes 2097168 | tf_op jit(solution)/shard_map/all_gather | solution.py:246
  62.7 2.6 fusion.105
  68.9 201.5 %all-gather.8.cloned.1.call-done = bf16[4096,1280]{0,1:T(8,128)(2,1)} async-done(((bf16[512,1280]{0,1:T(8,128)(2,1)}), bf16[4096,1280]{0,1:T(8,128)(2,1)}) %all-gather.8.cloned.1.call-update) | async-done | bytes 10485776 | tf_op jit(solution)/shard_map/all_gather | solution.py:19
  275.2 5.2 fusion.350
  308.5 79.9 %reduce-scatter.4.cloned.1.call-done = bf16[16,8192]{1,0:T(8,128)(2,1)} async-done(((bf16[256,8192]{1,0:T(8,128)(2,1)}), bf16[16,8192]{1,0:T(8,128)(2,1)}) %reduce-scatter.4.cloned.1.call-update) | async-done | bytes 262160 | tf_op jit(solution)/shard_map/reduce_scatter | solution.py:58
  391.9 4.1 copy.64
  396.0 52.8 %all-gather.10.cloned.1.call-done = bf16[256,8192]{1,0:T(8,128)(2,1)} async-done(((bf16[16,8192]{1,0:T(8,128)(2,1)}), bf16[256,8192]{1,0:T(8,128)(2,1)}) %all-gather.10.cloned.1.call-update) | async-done | bytes 4194320 | tf_op jit(solution)/shard_map/all_gather | solution.py:30
  448.9 2.6 fusion.91
  484.6 2.5 fusion.13
  489.5 4.4 all-to-all-start
  494.0 10.1 %all-gather.12.cloned.1.call-start = ((), (), s32[]{:S(2)}) async-start(), calls=%async_computation.9 | async-start | bytes 2228224 | tf_op jit(solution)/shard_map/all_gather | solution.py:327
  505.2 17.3 %all-to-all-done = bf16[16,16,4096]{2,1,0:T(8,128)(2,1)} async-done(((bf16[16,16,4096]{2,1,0:T(8,128)(2,1)}), bf16[16,16,4096]{2,1,0:T(8,128)(2,1)}, u32[]{:S(2)}, u32[]{:S(2)}) %all-to-all-start) | async-done | bytes 2097184 | tf_op jit(solution)/shard_map/all_to_all | solution.py:47
  526.1 48.3 %all-gather.12.cloned.1.call-done = bf16[256,4096]{1,0:T(8,128)(2,1)} async-done(((bf16[16,4096]{1,0:T(8,128)(2,1)}), bf16[256,4096]{1,0:T(8,128)(2,1)}) %all-gather.12.cloned.1.call-update) | async-done | bytes 2097168 | tf_op jit(solution)/shard_map/all_gather | solution.py:327
  574.4 3.6 fusion.71
  582.2 2.6 convolution_bitcast_fusion.5
  584.8 2.6 convolution_bitcast_fusion.1
  596.2 4.6 all-to-all-start.1
  608.3 3.8 reshape_reshape.21
  620.1 2.8 reshape_reshape.22
  623.0 2.9 fusion.9
  632.8 19.3 %pad_maximum_fusion.1 = bf16[8,327680]{1,0:T(8,128)(2,1)} fusion(bf16[8,131072]{1,0:T(8,128)(2,1)} %bitcast.295, bf16[8,32768]{1,0:T(8,128)(2,1)S(1)} %copy-done.19, bf16[8,32768]{1,0:T(8,128)(2,1)S(1)} %copy-done.18, bf16[8,131072]{1,0:T(8,128)(2,1)} %reshape_reshape.21), kind=kLoop, calls=%fused_computation.9 | loop fusion | flops 20971520 | bytes 10485760 | tf_op jit(solution)/shard_map/concatenate | solution.py:65
  652.0 7.2 reshape.1041
  659.3 22.8 %all-gather.14.cloned.1.call-done = bf16[256,4096]{1,0:T(8,128)(2,1)} async-done(((bf16[16,4096]{1,0:T(8,128)(2,1)}), bf16[256,4096]{1,0:T(8,128)(2,1)}) %all-gather.14.cloned.1.call-update) | async-done | bytes 2097168 | tf_op jit(solution)/shard_map/all_gather | solution.py:327
  682.1 3.0 fusion.68
  699.5 3.9 reshape_reshape.18
  708.3 2.8 reshape_reshape.20
  715.7 16.9 %pad_maximum_fusion = bf16[8,327680]{1,0:T(8,128)(2,1)} fusion(bf16[8,131072]{1,0:T(8,128)(2,1)S(1)} %bitcast.294, bf16[8,32768]{1,0:T(8,128)(2,1)} %reshape_reshape.20, bf16[8,32768]{1,0:T(8,128)(2,1)} %reshape_reshape.19, bf16[8,131072]{1,0:T(8,128)(2,1)} %reshape_reshape.18), kind=kLoop, calls=%fused_computation.8 | loop fusion | flops 20971520 | bytes 10485760 | tf_op jit(solution)/shard_map/concatenate | solution.py:65
  732.7 7.3 reshape.1038
  740.0 53.7 %reduce-scatter.8.cloned.1.call-done = bf16[2560,128]{1,0:T(8,128)(2,1)} async-done(((bf16[20480,128]{1,0:T(8,128)(2,1)}), bf16[2560,128]{1,0:T(8,128)(2,1)}) %reduce-scatter.8.cloned.1.call-update) | async-done | bytes 655376 | tf_op jit(solution)/shard_map/reduce_scatter | solution.py:68
  796.1 111.0 %reduce-scatter.6.cloned.1.call-done = bf16[2560,128]{1,0:T(8,128)(2,1)} async-done(((bf16[20480,128]{1,0:T(8,128)(2,1)}), bf16[2560,128]{1,0:T(8,128)(2,1)}) %reduce-scatter.6.cloned.1.call-update) | async-done | bytes 655376 | tf_op jit(solution)/shard_map/reduce_scatter | solution.py:68
  (316 shorter events, 157.7 us)
Async XLA Ops:
  7.2 55.5 %all-gather.6.cloned.1.call-start = ((), (), s32[]{:S(2)}) async-start(), calls=%async_computation.5 | async-start | bytes 2228224 | tf_op jit(solution)/shard_map/all_gather | solution.py:246
  10.8 259.6 %all-gather.8.cloned.1.call-start = ((), (), s32[]{:S(2)}) async-start(), calls=%async_computation.6 | async-start | bytes 11796480 | tf_op jit(solution)/shard_map/all_gather | solution.py:19
  14.4 373.9 %reduce-scatter.4.cloned.1.call-start = ((), (), s32[]{:S(2)}) async-start(), calls=%async_computation.7 | async-start | bytes 4456448 | tf_op jit(solution)/shard_map/reduce_scatter | solution.py:58
  18.3 47.3 %copy-start.12 = (bf16[2,4096,64]{1,2,0:T(8,128)(2,1)S(1)}, bf16[2,4096,64]{1,2,0:T(8,128)(2,1)}, u32[]{:S(2)}) copy-start(bf16[2,4096,64]{1,2,0:T(8,128)(2,1)} %param.15) | copy-start | bytes 3145732
  24.2 439.6 %copy-start.22 = (f32[256,64]{0,1:T(8,128)}, f32[256,64]{0,1:T(8,128)S(1)}, u32[]{:S(2)}) copy-start(f32[256,64]{0,1:T(8,128)S(1)} %get-tuple-element.175) | copy-start | bytes 196612
  65.3 2.9 collective-permute-start.1
  66.4 2.5 collective-permute-start
  273.5 22.7 %collective-permute-start.3 = (bf16[256,64]{0,1:T(8,128)(2,1)}, bf16[256,64]{0,1:T(8,128)(2,1)}, u32[]{:S(2)}, u32[]{:S(2)}) collective-permute-start(bf16[256,64]{0,1:T(8,128)(2,1)} %fusion.92), channel_id=1, source_target_pairs={{0,1},{1,0},{2,3},{3,2},{4,5},{5,4},{6,7},{7,6},{8,9},{9,8},{10,11... | collective-permute-start | bytes 98312 | tf_op jit(solution)/shard_map/ppermute | solution.py:37
  275.1 9.0 collective-permute-start.2
  284.1 13.6 %copy-start.37 = (bf16[256,2,64]{0,2,1:T(8,128)(2,1)}, bf16[256,2,64]{0,2,1:T(8,128)(2,1)S(1)}, u32[]{:S(2)}) copy-start(bf16[256,2,64]{0,2,1:T(8,128)(2,1)S(1)} %get-tuple-element.153) | copy-start | bytes 196612
  284.1 13.6 %copy-start.39 = (bf16[256,2,64]{0,2,1:T(8,128)(2,1)}, bf16[256,2,64]{0,2,1:T(8,128)(2,1)S(1)}, u32[]{:S(2)}) copy-start(bf16[256,2,64]{0,2,1:T(8,128)(2,1)S(1)} %get-tuple-element.154) | copy-start | bytes 196612
  296.2 7.3 copy-start.26
  308.2 80.2 %copy-start.30 = (bf16[16,4096]{1,0:T(8,128)(2,1)S(1)}, bf16[16,4096]{1,0:T(8,128)(2,1)}, u32[]{:S(2)}) copy-start(bf16[16,4096]{1,0:T(8,128)(2,1)} %param.11) | copy-start | bytes 393220
  308.2 140.7 %all-gather.10.cloned.1.call-start = ((), (), s32[]{:S(2)}) async-start(), calls=%async_computation.8 | async-start | bytes 4456448 | tf_op jit(solution)/shard_map/all_gather | solution.py:30
  453.9 10.6 %collective-permute-start.6 = (bf16[256,64]{0,1:T(8,128)(2,1)S(1)}, bf16[256,64]{0,1:T(8,128)(2,1)S(1)}, u32[]{:S(2)}, u32[]{:S(2)}) collective-permute-start(bf16[256,64]{0,1:T(8,128)(2,1)S(1)} %get-tuple-element.186), channel_id=1, source_target_pairs={{0,1},{1,0},{2,3},{3,2},{4,5},{5,4},{6,7},{7,6},{8,9},{9,8},{10,11... | collective-permute-start | bytes 98312 | tf_op jit(solution)/shard_map/ppermute | solution.py:37
  455.1 9.5 %collective-permute-start.4 = (bf16[256,64]{0,1:T(8,128)(2,1)S(1)}, bf16[256,64]{0,1:T(8,128)(2,1)S(1)}, u32[]{:S(2)}, u32[]{:S(2)}) collective-permute-start(bf16[256,64]{0,1:T(8,128)(2,1)S(1)} %fusion.103), channel_id=1, source_target_pairs={{0,1},{1,0},{2,3},{3,2},{4,5},{5,4},{6,7},{7,6},{8,9},{9,8},{10,11... | collective-permute-start | bytes 98312 | tf_op jit(solution)/shard_map/ppermute | solution.py:37
  457.5 23.3 %collective-permute-start.7 = (bf16[256,64]{0,1:T(8,128)(2,1)}, bf16[256,64]{0,1:T(8,128)(2,1)}, u32[]{:S(2)}, u32[]{:S(2)}) collective-permute-start(bf16[256,64]{0,1:T(8,128)(2,1)} %fusion.79), channel_id=1, source_target_pairs={{0,1},{1,0},{2,3},{3,2},{4,5},{5,4},{6,7},{7,6},{8,9},{9,8},{10,11... | collective-permute-start | bytes 98312 | tf_op jit(solution)/shard_map/ppermute | solution.py:37
  459.2 6.1 collective-permute-start.5
  480.8 6.3 copy-start.33
  489.5 32.9 %all-to-all-start = ((bf16[16,16,4096]{2,1,0:T(8,128)(2,1)}), bf16[16,16,4096]{2,1,0:T(8,128)(2,1)}, u32[]{:S(2)}, u32[]{:S(2)}) async-start(bf16[16,16,4096]{2,1,0:T(8,128)(2,1)} %bitcast.299), calls=%async_computation.1 | async-start | bytes 4194304 | tf_op jit(solution)/shard_map/all_to_all | solution.py:47
  494.0 80.4 %all-gather.12.cloned.1.call-start = ((), (), s32[]{:S(2)}) async-start(), calls=%async_computation.9 | async-start | bytes 2228224 | tf_op jit(solution)/shard_map/all_gather | solution.py:327
  590.2 3.5 collective-permute-start.9
  590.9 2.0 collective-permute-start.8
  596.2 33.1 %all-to-all-start.1 = ((bf16[16,16,4096]{2,1,0:T(8,128)(2,1)}), bf16[16,16,4096]{2,1,0:T(8,128)(2,1)}, u32[]{:S(2)}, u32[]{:S(2)}) async-start(bf16[16,16,4096]{2,1,0:T(8,128)(2,1)} %bitcast.296), calls=%async_computation.2 | async-start | bytes 4194304 | tf_op jit(solution)/shard_map/all_to_all | solution.py:47
  600.8 81.3 %all-gather.14.cloned.1.call-start = ((), (), s32[]{:S(2)}) async-start(), calls=%async_computation.10 | async-start | bytes 2228224 | tf_op jit(solution)/shard_map/all_gather | solution.py:327
  632.3 161.4 %reduce-scatter.8.cloned.1.call-start = ((), (), s32[]{:S(2)}) async-start(), calls=%async_computation.12 | async-start | bytes 5898240 | tf_op jit(solution)/shard_map/reduce_scatter | solution.py:68
  659.3 25.8 %copy-start.38 = (bf16[256,2,64]{0,2,1:T(8,128)(2,1)S(1)}, bf16[256,2,64]{0,2,1:T(8,128)(2,1)}, u32[]{:S(2)}) copy-start(bf16[256,2,64]{0,2,1:T(8,128)(2,1)} %copy-done.37) | copy-start | bytes 196612
  659.3 25.8 %copy-start.40 = (bf16[256,2,64]{0,2,1:T(8,128)(2,1)S(1)}, bf16[256,2,64]{0,2,1:T(8,128)(2,1)}, u32[]{:S(2)}) copy-start(bf16[256,2,64]{0,2,1:T(8,128)(2,1)} %copy-done.39) | copy-start | bytes 196612
  659.3 25.8 %copy-start.48 = (bf16[256,128]{0,1:T(8,128)(2,1)S(1)}, bf16[256,128]{0,1:T(8,128)(2,1)}, u32[]{:S(2)}) copy-start(bf16[256,128]{0,1:T(8,128)(2,1)} %copy-done.47) | copy-start | bytes 196612
  659.3 247.8 %reduce-scatter.6.cloned.1.call-start = ((), (), s32[]{:S(2)}) async-start(), calls=%async_computation.11 | async-start | bytes 5898240 | tf_op jit(solution)/shard_map/reduce_scatter | solution.py:68
  694.4 9.1 collective-permute-start.11
  695.2 16.0 %collective-permute-start.10 = (bf16[256,64]{0,1:T(8,128)(2,1)S(1)}, bf16[256,64]{0,1:T(8,128)(2,1)S(1)}, u32[]{:S(2)}, u32[]{:S(2)}) collective-permute-start(bf16[256,64]{0,1:T(8,128)(2,1)S(1)} %get-tuple-element.88), channel_id=1, source_target_pairs={{0,1},{1,0},{2,3},{3,2},{4,5},{5,4},{6,7},{7,6},{8,9},{9,8},{10,11... | collective-permute-start | bytes 98312 | tf_op jit(solution)/shard_map/ppermute | solution.py:37
  (59 other events, 155.6 us)
Sparse Core Ops, SparseCore 0:
  10.9 51.6 all-gather.5
  64.3 206.0 all-gather.7
  308.3 80.0 reduce-scatter.3
  392.0 56.7 all-gather.9
  526.2 48.1 all-gather.11
  632.4 49.6 all-gather.13
  684.5 109.1 reduce-scatter.7
  796.1 111.0 reduce-scatter.5
where the time goes:
time: 932 us; the launch traced here: 921 us
  waiting for transfers between devices  626 us (67%)
  matrix products  104 us (11%)
  local copies, waits for them, and re-layouts  81 us (9%)
  other arithmetic  70.1 us (8%)
  starting transfers between devices  24.2 us (3%)
  between operations  15.4 us (2%)
    all_gather x1, waiting for transfers between devices, turned_gather(): result, at, done = (lax.all_gather(both, axis, axis=0, tiled=True), 0, [])  201 us
    reduce_scatter x2, waiting for transfers between devices, sum_packed(): lax.psum_scatter(lines, axis, tiled=True).reshape(-1)  165 us
    reduce_scatter x1, waiting for transfers between devices, side_by_side(): lax.psum_scatter(both, axis, scatter_dimension=dim, tiled=True)  79.9 us
    all_gather x2, waiting for transfers between devices, body(): cotangent_low = lax.all_gather(cotangent_low, 'tensor', axis=0, tiled=True)  71.1 us
    all_gather x1, waiting for transfers between devices, sent_together(): result = lax.all_gather(both, axis, axis=dim, tiled=True)  52.8 us
    all_gather x1, waiting for transfers between devices, body(): normed_all = lax.all_gather(normed, 'tensor', axis=0, tiled=True)  38.5 us
    concatenate x2, other arithmetic, sum_packed(): lines = jnp.concatenate([b.reshape(length, -1) for b in pieces], axis=1)  36.2 us
    dot_general x20, matrix products, multiply(): jnp.einsum(pattern, left_side, right_side, preferred_element_type=jnp.flo...  35.1 us
  transfers between devices with their start and end apart: 22, of which 10 were waited for; matrix products, arithmetic and copies ran while one was open for 20% of the time, Pallas kernels for 0%

commit v1 on v0

v1 whole, which is shorter than its diff:
```python
import functools
import math

import jax
import jax.numpy as jnp
from jax import lax
from jax.experimental import pallas as pl
from jax.experimental.pallas import tpu as pltpu
from jax.sharding import Mesh
from jax.sharding import PartitionSpec as P

HD = 128
LEN = 256
EPS = 1e-05
THETA = 500000.0
DP = ("z", "y")
CHIPS = ("x", "w")
BF = jnp.bfloat16
F32 = jnp.float32


def matmul(left_side, right_side):
    return jnp.dot(left_side, right_side, preferred_element_type=F32)


def contract_rows(left_side, right_side):
    return lax.dot_general(
        left_side, right_side, (((0,), (0,)), ((), ())), preferred_element_type=F32
    )


def contract_last(left_side, right_side):
    return lax.dot_general(
        left_side, right_side, (((1,), (1,)), ((), ())), preferred_element_type=F32
    )


def core_swap(value):
    return lax.ppermute(value, "c", [(0, 1), (1, 0)])


def exchange(pieces, axis):
    return lax.all_to_all(pieces, axis, split_axis=0, concat_axis=0, tiled=True)


def copies(value, axis):
    return jnp.broadcast_to(value[None], (lax.axis_size(axis),) + value.shape)


def gather_rows(share):
    mine = exchange(copies(share, CHIPS), CHIPS).reshape(-1, share.shape[-1])
    return (mine, core_swap(mine))


def sum_rows(own_half, other_half):
    pair = own_half + core_swap(other_half.astype(BF)).astype(F32)
    chips = lax.axis_size(CHIPS)
    pieces = pair.astype(BF).reshape(chips, -1, pair.shape[-1])
    return exchange(pieces, CHIPS).astype(F32).sum(axis=0)


def rope(values, cosine, sine, turn):
    return values * cosine + turn(values) * sine


def half_turn(values):
    return pltpu.roll(values, values.shape[1] // 2, 1)


def attend_kernel(
    size_ref,
    core_ref,
    query_ref,
    own_ref,
    other_ref,
    tangent_query_ref,
    tangent_own_ref,
    tangent_other_ref,
    cosine_ref,
    sine_ref,
    row_ref,
    column_ref,
    blended_ref,
    tangent_ref,
    queries_ref,
    keys_ref,
    values_ref,
    weights_ref,
):
    size = size_ref[0]
    low_core = core_ref[0] == 0
    cosine = cosine_ref[...]
    sine = sine_ref[...]
    lane = lax.broadcasted_iota(jnp.int32, own_ref.shape, 1)
    lower = lane < HD // 2

    def join(own, other):
        first = jnp.where(low_core, own, other)
        second = jnp.where(low_core, other, own)
        key = jnp.where(lower, first, half_turn(second))
        value = jnp.where(lower, half_turn(first), second)
        return rope(key, cosine, sine, half_turn).astype(BF), value.astype(BF)

    key, value = join(own_ref[...], other_ref[...].astype(F32))
    tangent_key, tangent_value = join(tangent_own_ref[...], tangent_other_ref[...].astype(F32))
    keys_ref[...] = key
    values_ref[...] = value
    rows = row_ref[...]
    columns = column_ref[...]
    allowed = (columns <= rows) & (columns < size)
    scaling = 1.0 / math.sqrt(HD)
    for head in range(query_ref.shape[1] // HD):
        at = slice(head * HD, (head + 1) * HD)
        query = rope(query_ref[:, at], cosine, sine, half_turn).astype(BF)
        tangent_query = rope(tangent_query_ref[:, at], cosine, sine, half_turn).astype(BF)
        scores = contract_last(query, key) * scaling
        powers = jnp.where(allowed, jnp.exp(scores), 0.0)
        weights = powers / jnp.sum(powers, axis=-1, keepdims=True)
        weights_low = weights.astype(BF)
        blended_ref[:, at] = matmul(weights_low, value).astype(BF)
        tangent_scores = (
            contract_last(tangent_query, key) + contract_last(query, tangent_key)
        ) * scaling
        shift = jnp.sum(weights * tangent_scores, axis=-1, keepdims=True)
        tangent_weights = (weights * (tangent_scores - shift)).astype(BF)
        tangent_ref[:, at] = (
            matmul(tangent_weights, value) + matmul(weights_low, tangent_value)
        ).astype(BF)
        queries_ref[:, at] = query
        weights_ref[head] = weights


def attend(size, core, query, own, other, tangent_query, tangent_own, tangent_other, tables):
    rows, width = query.shape
    wide = jax.ShapeDtypeStruct((rows, width), BF)
    narrow = jax.ShapeDtypeStruct((rows, HD), BF)
    weights = jax.ShapeDtypeStruct((width // HD, rows, rows), F32)
    smem = pl.BlockSpec(memory_space=pltpu.SMEM)
    vmem = pl.BlockSpec(memory_space=pltpu.VMEM)
    return pl.pallas_call(
        attend_kernel,
        out_shape=(wide, wide, wide, narrow, narrow, weights),
        in_specs=[smem] * 2 + [vmem] * 10,
        out_specs=(vmem,) * 6,
        name="attend",
    )(size, core, query, own, other, tangent_query, tangent_own, tangent_other, *tables)


def attend_back_kernel(
    weights_ref,
    queries_ref,
    keys_ref,
    values_ref,
    grad_ref,
    cosine_ref,
    sine_ref,
    grad_query_ref,
    grad_key_ref,
    grad_value_ref,
):
    cosine = cosine_ref[...]
    sine = -sine_ref[...]
    key = keys_ref[...]
    value = values_ref[...]
    scaling = 1.0 / math.sqrt(HD)
    grad_key = jnp.zeros(key.shape, F32)
    grad_value = jnp.zeros(value.shape, F32)
    for head in range(queries_ref.shape[1] // HD):
        at = slice(head * HD, (head + 1) * HD)
        weights = weights_ref[head]
        grad = grad_ref[:, at]
        grad_weights = contract_last(grad, value)
        grad_value = grad_value + contract_rows(weights.astype(BF), grad)
        shift = jnp.sum(weights * grad_weights, axis=-1, keepdims=True)
        grad_scores = (weights * (grad_weights - shift) * scaling).astype(BF)
        grad_query_ref[:, at] = rope(
            matmul(grad_scores, key), cosine, sine, half_turn
        ).astype(BF)
        grad_key = grad_key + contract_rows(grad_scores, queries_ref[:, at])
    grad_key_ref[...] = rope(grad_key, cosine, sine, half_turn).astype(BF)
    grad_value_ref[...] = grad_value.astype(BF)


def attend_back(weights, queries, keys, values, grad, cosine, sine):
    vmem = pl.BlockSpec(memory_space=pltpu.VMEM)
    return pl.pallas_call(
        attend_back_kernel,
        out_shape=(
            jax.ShapeDtypeStruct(queries.shape, BF),
            jax.ShapeDtypeStruct(keys.shape, BF),
            jax.ShapeDtypeStruct(values.shape, BF),
        ),
        in_specs=[vmem] * 7,
        out_specs=(vmem,) * 3,
        name="attend_back",
    )(weights, queries, keys, values, grad, cosine, sine)


def normalize(stream, gain_row):
    wide_stream = stream.astype(F32)
    inverse = lax.rsqrt(jnp.mean(wide_stream * wide_stream, axis=-1, keepdims=True) + EPS)
    return (wide_stream, inverse, (wide_stream * inverse * gain_row).astype(BF))


def norm_tangent(wide_stream, inverse, tangent, gain_row):
    shift = jnp.mean(wide_stream * tangent, axis=-1, keepdims=True)
    return (
        gain_row * (tangent * inverse - wide_stream * inverse * inverse * inverse * shift)
    ).astype(BF)


def norm_back(wide_stream, inverse, grad_normed, gain_row):
    scaled = grad_normed * gain_row
    shift = jnp.mean(wide_stream * scaled, axis=-1, keepdims=True)
    return inverse * (scaled - wide_stream * inverse * inverse * shift)


def body(
    tokens,
    lengths,
    norm_gains,
    query_weight,
    key_weight,
    value_weight,
    out_weight,
    query_probe,
    key_probe,
    value_probe,
    out_probe,
):
    share_rows, features = tokens.shape
    layer_count, query_width = query_weight.shape[0], query_weight.shape[2]
    half_width = key_weight.shape[2]
    batches = lax.axis_size(DP)
    core = lax.axis_index("c")
    chip = lax.axis_index(CHIPS)
    low_core = core == 0
    rows = LEN
    half = rows // 2
    size = lax.dynamic_slice_in_dim(lengths, lax.axis_index(DP), 1)
    core_word = core.astype(jnp.int32).reshape(1)

    number = jnp.arange(rows)
    owner = jnp.where(number < half, core, 1 - core)
    within = number % half
    position = (within // share_rows) * (2 * share_rows) + owner * share_rows + within % share_rows
    column = jnp.arange(HD // 2).astype(F32)
    frequency = jnp.exp(-math.log(THETA) * 2.0 * column / HD)
    angles = position.astype(F32)[:, None] * frequency[None, :]
    cosine = jnp.concatenate([jnp.cos(angles)] * 2, axis=1)
    sine = jnp.concatenate([-jnp.sin(angles), jnp.sin(angles)], axis=1)
    position = position.astype(jnp.int32)
    tables = (cosine, sine, position[:, None], position[None, :])
    share_position = (chip * 2 + core) * share_rows + jnp.arange(share_rows)
    share_mask = (share_position < size[0]).astype(F32)

    def turned(values):
        return jnp.concatenate([values[half:], values[:half]], axis=0)

    weights = [
        jnp.concatenate([query_weight[n], key_weight[n], value_weight[n]], axis=1)
        for n in range(layer_count)
    ]
    probes = [
        jnp.concatenate([query_probe[n], key_probe[n], value_probe[n]], axis=1)
        for n in range(layer_count)
    ]
    out_turned = [out_probe[n].T for n in range(layer_count)]
    full_probes = [None] * layer_count
    full_out = [None] * layer_count
    full_probes[0] = exchange(copies(probes[0], DP), DP).reshape(features, -1)
    for n in range(layer_count):
        if n > 0:
            full_probes[n] = lax.all_gather(probes[n], DP, axis=0, tiled=True)
        full_out[n] = lax.all_gather(out_turned[n], DP, axis=0, tiled=True)

    stream = tokens
    tangent = None
    stored = []
    all_rows = None
    for n in range(layer_count):
        final_layer = n == layer_count - 1
        gain_row = norm_gains[n]
        wide_stream, inverse, normed = normalize(stream, gain_row)
        if tangent is None:
            normed_halves = gather_rows(normed)
            both = jnp.concatenate(normed_halves, axis=0)
            primal = matmul(both, weights[n])
            moved = matmul(both, full_probes[n])
        else:
            tangent_normed = norm_tangent(wide_stream, inverse, tangent, gain_row)
            joined = gather_rows(jnp.concatenate([normed, tangent_normed], axis=1))
            both = jnp.concatenate([part[:, :features] for part in joined], axis=0)
            tangent_both = jnp.concatenate([part[:, features:] for part in joined], axis=0)
            primal = matmul(both, weights[n])
            moved = matmul(both, full_probes[n]) + matmul(tangent_both, weights[n])
        if n == 0:
            pieces = jnp.moveaxis(both.reshape(rows, batches, -1), 1, 0)
            all_rows = exchange(pieces, DP).reshape(batches * rows, -1)
        own = jnp.concatenate([primal[:, query_width:], moved[:, query_width:]], axis=1)
        other = turned(core_swap(own.astype(BF)))
        blended, tangent_blended, queries, keys, values, attention = attend(
            size,
            core_word,
            primal[:, :query_width],
            own[:, :HD],
            other[:, :HD],
            moved[:, :query_width],
            own[:, HD:],
            other[:, HD:],
            tables,
        )

        def out_terms(at):
            moved_part = matmul(tangent_blended[at], out_weight[n]) + contract_last(
                blended[at], full_out[n]
            )
            if final_layer:
                return moved_part
            return jnp.concatenate([matmul(blended[at], out_weight[n]), moved_part], axis=1)

        other_terms = out_terms(slice(half, rows))
        own_terms = out_terms(slice(0, half))
        sums = sum_rows(own_terms, other_terms)
        stored.append((wide_stream, inverse, both, queries, keys, values, blended, attention))
        if final_layer:
            tangent_sum = sums
        else:
            stream = (wide_stream + sums[:, :features]).astype(BF)
            tangent_sum = sums[:, features:]
        tangent = tangent_sum if tangent is None else tangent + tangent_sum
    cotangent = share_mask[:, None] * tangent
    projected = [None] * layer_count
    out_products = [None] * layer_count
    for n in reversed(range(layer_count)):
        wide_stream, inverse, both, queries, keys, values, blended, attention = stored[n]
        cotangent_both = jnp.concatenate(gather_rows(cotangent.astype(BF)), axis=0)
        grad_mixed = contract_last(cotangent_both, out_weight[n]).astype(BF)
        out_term = contract_rows(cotangent_both, blended).astype(BF)
        out_products[n] = lax.psum_scatter(out_term, DP, scatter_dimension=0, tiled=True)
        query_low, key_low, value_low = attend_back(
            attention, queries, keys, values, grad_mixed, cosine, sine
        )
        key_value = jnp.concatenate([key_low, value_low], axis=1).reshape(rows, 2, 2, half_width)
        own_part = jnp.where(low_core, key_value[:, :, 0], key_value[:, :, 1])
        other_part = jnp.where(low_core, key_value[:, :, 1], key_value[:, :, 0])
        arrived = turned(core_swap(other_part.reshape(rows, -1)))
        pair = (own_part.reshape(rows, -1).astype(F32) + arrived.astype(F32)).astype(BF)
        grads = jnp.concatenate([query_low, pair], axis=1)
        if n > 0:
            own_terms = contract_last(grads[:half], weights[n])
            other_terms = contract_last(grads[half:], weights[n])
            grad_normed = sum_rows(own_terms, other_terms)
            cotangent = cotangent + norm_back(wide_stream, inverse, grad_normed, norm_gains[n])
            term = contract_rows(both, grads).astype(BF)
            projected[n] = lax.psum_scatter(term, DP, scatter_dimension=0, tiled=True).astype(F32)
        else:
            all_grads = exchange(copies(grads, DP), DP).reshape(batches * rows, -1)
            projected[n] = contract_rows(all_rows, all_grads)
    projected = jnp.stack(projected)
    key_end = query_width + half_width
    out_stack = jnp.stack([product.astype(F32).T for product in out_products])
    return (
        projected[:, :, :query_width],
        projected[:, :, query_width:key_end],
        projected[:, :, key_end:],
        out_stack,
    )


def solution(mesh):
    inner = Mesh(mesh.devices.reshape(4, 2, 4, 2, 2), ("z", "y", "x", "w", "c"))
    tensor = ("x", "w", "c")
    placed = (
        P(DP + tensor, None),
        P(),
        P(),
        P(None, None, tensor),
        P(None, None, tensor),
        P(None, None, tensor),
        P(None, tensor, None),
        P(None, DP, tensor),
        P(None, DP, tensor),
        P(None, DP, tensor),
        P(None, tensor, DP),
    )
    return jax.shard_map(
        body,
        mesh=inner,
        in_specs=placed,
        out_specs=(
            P(None, DP, tensor),
            P(None, DP, tensor),
            P(None, DP, tensor),
            P(None, tensor, DP),
        ),
        check_vma=False,
    )
```

time: 932 us -> 612 us (0.66); the launches traced: 921 us -> 611 us
  waiting for transfers between devices: 626 us -> 313 us
  blocking collectives: 0 us -> 112 us
  matrix products: 104 us -> 49.6 us
  other arithmetic: 70.1 us -> 18.5 us
  local copies, waits for them, and re-layouts: 81 us -> 43.7 us
  starting transfers between devices: 24.2 us -> 44.3 us
  Pallas kernels: 0 us -> 14.8 us
    all_gather x5 -> x3, waiting for transfers between devices: 364 us -> 62.5 us  [the longest x2 38.9 us: body(): full_out[n] = lax.all_gather(out_turned[n], DP, axis=0, tiled=True)]
    reduce_scatter x3, waiting for transfers between devices: 245 us -> 80.2 us  [the longest x2 80.1 us: body(): lax.psum_scatter(out_term, DP, scatter_dimension=0, tiled=True)]
    all_to_all x2 -> x6, waiting for transfers between devices: 17.5 us -> 161 us  [exchange(): return lax.all_to_all(pieces, axis, split_axis=0, concat_axis=0, tiled=True)]
    all_to_all x0 -> x4, blocking collectives: none -> 112 us  [exchange(): return lax.all_to_all(pieces, axis, split_axis=0, concat_axis=0, tiled=True)]
    dot_general x40 -> x11, matrix products: 63.1 us -> 19.9 us  [matmul(): return jnp.dot(left_side, right_side, preferred_element_type=F32)]
    concatenate x18 -> x12, other arithmetic: 48.1 us -> 6.08 us  [the longest x2 1.77 us: body(): jnp.concatenate([key_low, value_low], axis=1)]
    all_to_all x2 -> x6, starting transfers between devices: 9.01 us -> 32.3 us  [exchange(): return lax.all_to_all(pieces, axis, split_axis=0, concat_axis=0, tiled=True)]
    another operation x6 -> x0, local copies, waits for them, and re-layouts: 16.7 us -> none  [sum_packed(): lines = jnp.concatenate([b.reshape(length, -1) for b in pieces], axis=1)]
  transfers between devices with their start and end apart: 22 -> 23, of which waited for: 10 -> 16; matrix products, arithmetic and copies ran while one was open for 20% -> 13% of each run, Pallas kernels for 0% -> 2%
where the time goes in v1:
time: 612 us; the launch traced here: 611 us
  waiting for transfers between devices  313 us (51%)
  blocking collectives  112 us (18%)
  matrix products  49.6 us (8%)
  starting transfers between devices  44.3 us (7%)
  local copies, waits for them, and re-layouts  43.7 us (7%)
  other arithmetic  18.5 us (3%)
  between operations  14.9 us (2%)
  Pallas kernels  14.8 us (2%)
    all_to_all x6, waiting for transfers between devices, exchange(): return lax.all_to_all(pieces, axis, split_axis=0, concat_axis=0, tiled=True)  161 us
    all_to_all x4, blocking collectives, exchange(): return lax.all_to_all(pieces, axis, split_axis=0, concat_axis=0, tiled=True)  112 us
    reduce_scatter x2, waiting for transfers between devices, body(): lax.psum_scatter(out_term, DP, scatter_dimension=0, tiled=True)  80.1 us
    all_gather x2, waiting for transfers between devices, body(): full_out[n] = lax.all_gather(out_turned[n], DP, axis=0, tiled=True)  38.9 us
    all_to_all x6, starting transfers between devices, exchange(): return lax.all_to_all(pieces, axis, split_axis=0, concat_axis=0, tiled=True)  32.3 us
    all_gather x1, waiting for transfers between devices, body(): full_probes[n] = lax.all_gather(probes[n], DP, axis=0, tiled=True)  23.5 us
    dot_general x11, matrix products, matmul(): return jnp.dot(left_side, right_side, preferred_element_type=F32)  19.9 us
    dot_general x8, matrix products, contract_last(): lax.dot_general(left_side, right_side, (((1,), (1,)), ((), ())), preferre...  18.1 us
  transfers between devices with their start and end apart: 23, of which 16 were waited for; matrix products, arithmetic and copies ran while one was open for 13% of the time, Pallas kernels for 2%

profile of v1, /device:TPU:1, one launch (start us, length us, event | category | flops | bytes accessed | tf_op | source)
XLA Modules:
  0.0 610.8 jit_solution(13233926070242788604)
XLA Ops:
  11.2 7.5 %all-to-all-start = ((bf16[8,16,4096]{2,1,0:T(8,128)(2,1)}), bf16[8,16,4096]{2,1,0:T(8,128)(2,1)S(1)}, u32[]{:S(2)}, u32[]{:S(2)}) async-start(bf16[8,16,4096]{2,1,0:T(8,128)(2,1)} %broadcast_in_dim.28), calls=%async_computation | async-start | bytes 2097152 | tf_op jit(solution)/shard_map/all_to_all | solution.py:43
  23.8 10.5 %all-to-all-done = bf16[8,16,4096]{2,1,0:T(8,128)(2,1)S(1)} async-done(((bf16[8,16,4096]{2,1,0:T(8,128)(2,1)}), bf16[8,16,4096]{2,1,0:T(8,128)(2,1)S(1)}, u32[]{:S(2)}, u32[]{:S(2)}) %all-to-all-start) | async-done | bytes 1048608 | tf_op jit(solution)/shard_map/all_to_all | solution.py:43
  36.3 5.2 all-to-all-start.2
  47.7 3.9 slice_bitcast_fusion
  53.1 56.6 %all-to-all-done.2 = bf16[8,512,384]{2,1,0:T(8,128)(2,1)} async-done(((bf16[8,512,384]{2,1,0:T(8,128)(2,1)}), bf16[8,512,384]{2,1,0:T(8,128)(2,1)}, u32[]{:S(2)}, u32[]{:S(2)}) %all-to-all-start.2) | async-done | bytes 3145760 | tf_op jit(solution)/shard_map/all_to_all | solution.py:43
  109.7 3.5 fusion.31
  119.9 4.5 attend.2
  137.2 6.3 %all-to-all-start.3 = ((bf16[8,16,8192]{2,1,0:T(8,128)(2,1)}), bf16[8,16,8192]{2,1,0:T(8,128)(2,1)S(1)}, u32[]{:S(2)}, u32[]{:S(2)}) async-start(bf16[8,16,8192]{2,1,0:T(8,128)(2,1)} %bitcast.106), calls=%async_computation.3 | async-start | bytes 4194304 | tf_op jit(solution)/shard_map/all_to_all | solution.py:43
  144.9 29.9 %all-to-all-done.3 = bf16[8,16,8192]{2,1,0:T(8,128)(2,1)S(1)} async-done(((bf16[8,16,8192]{2,1,0:T(8,128)(2,1)}), bf16[8,16,8192]{2,1,0:T(8,128)(2,1)S(1)}, u32[]{:S(2)}, u32[]{:S(2)}) %all-to-all-start.3) | async-done | bytes 2097184 | tf_op jit(solution)/shard_map/all_to_all | solution.py:43
  176.0 37.3 %all_to_all.50 = bf16[8,16,8192]{2,1,0:T(8,128)(2,1)S(1)} all-to-all(bf16[8,16,8192]{2,1,0:T(8,128)(2,1)S(1)} %broadcast_in_dim.36), channel_id=1, replica_groups=mesh['z'=4,'y'=2,'x'=4,'w'=2,'c'=2] {'x','w'}, dimensions={0} | all-to-all | bytes 4194304 | tf_op jit(solution)/shard_map/all_to_all | solution.py:43
  224.6 23.5 %all-gather.6.cloned.1.call-done = bf16[4096,384]{1,0:T(8,128)(2,1)} async-done(((bf16[512,384]{1,0:T(8,128)(2,1)}), bf16[4096,384]{1,0:T(8,128)(2,1)}) %all-gather.6.cloned.1.call-update) | async-done | bytes 3145744 | tf_op jit(solution)/shard_map/all_gather | solution.py:274
  248.2 4.0 convolution_add_fusion.4
  258.2 4.5 attend.3
  264.8 38.9 %all-gather.8.cloned.1.call-done = bf16[4096,256]{0,1:T(8,128)(2,1)} async-done(((bf16[512,256]{0,1:T(8,128)(2,1)}), bf16[4096,256]{0,1:T(8,128)(2,1)}) %all-gather.8.cloned.1.call-update) | async-done | bytes 2097168 | tf_op jit(solution)/shard_map/all_gather | solution.py:275
  311.4 6.1 %all-to-all-start.5 = ((bf16[8,16,4096]{2,1,0:T(8,128)(2,1)}), bf16[8,16,4096]{2,1,0:T(8,128)(2,1)S(1)}, u32[]{:S(2)}, u32[]{:S(2)}) async-start(bf16[8,16,4096]{2,1,0:T(8,128)(2,1)} %bitcast.28), calls=%async_computation.5 | async-start | bytes 2097152 | tf_op jit(solution)/shard_map/all_to_all | solution.py:43
  318.3 15.0 %all-to-all-done.5 = bf16[8,16,4096]{2,1,0:T(8,128)(2,1)S(1)} async-done(((bf16[8,16,4096]{2,1,0:T(8,128)(2,1)}), bf16[8,16,4096]{2,1,0:T(8,128)(2,1)S(1)}, u32[]{:S(2)}, u32[]{:S(2)}) %all-to-all-start.5) | async-done | bytes 1048608 | tf_op jit(solution)/shard_map/all_to_all | solution.py:43
  333.6 19.2 %all_to_all.51 = bf16[8,16,4096]{2,1,0:T(8,128)(2,1)S(1)} all-to-all(bf16[8,16,4096]{2,1,0:T(8,128)(2,1)S(1)} %broadcast_in_dim.70), channel_id=1, replica_groups=mesh['z'=4,'y'=2,'x'=4,'w'=2,'c'=2] {'x','w'}, dimensions={0} | all-to-all | bytes 2097152 | tf_op jit(solution)/shard_map/all_to_all | solution.py:43
  358.5 3.0 fusion.35.grad_ref
  361.5 3.0 attend_back.2
  367.8 3.6 convolution_convert_fusion
  380.8 3.7 all-to-all-start.7
  384.6 3.4 convolution_convert_fusion.1
  388.0 14.9 %all-to-all-done.7 = bf16[8,16,4096]{2,1,0:T(8,128)(2,1)S(1)} async-done(((bf16[8,16,4096]{2,1,0:T(8,128)(2,1)}), bf16[8,16,4096]{2,1,0:T(8,128)(2,1)S(1)}, u32[]{:S(2)}, u32[]{:S(2)}) %all-to-all-start.7) | async-done | bytes 1048608 | tf_op jit(solution)/shard_map/all_to_all | solution.py:43
  403.4 22.5 %all_to_all.52 = bf16[8,16,4096]{2,1,0:T(8,128)(2,1)} all-to-all(bf16[8,16,4096]{2,1,0:T(8,128)(2,1)S(1)} %broadcast_in_dim.71), channel_id=1, replica_groups=mesh['z'=4,'y'=2,'x'=4,'w'=2,'c'=2] {'x','w'}, dimensions={0} | all-to-all | bytes 2097152 | tf_op jit(solution)/shard_map/all_to_all | solution.py:43
  430.0 3.7 convolution_convert_fusion.2
  435.3 3.6 all-to-all-start.1
  438.9 3.7 fusion.32.grad_ref
  442.6 2.9 attend_back.3
  449.1 34.6 %all-to-all-done.1 = bf16[8,256,512]{2,1,0:T(8,128)(2,1)S(1)} async-done(((bf16[8,256,512]{2,1,0:T(8,128)(2,1)}), bf16[8,256,512]{2,1,0:T(8,128)(2,1)S(1)}, u32[]{:S(2)}, u32[]{:S(2)}) %all-to-all-start.1) | async-done | bytes 2097184 | tf_op jit(solution)/shard_map/all_to_all | solution.py:43
  483.8 33.3 %all_to_all.53 = bf16[8,256,384]{1,2,0:T(8,128)(2,1)S(1)} all-to-all(bf16[8,256,384]{1,2,0:T(8,128)(2,1)S(1)} %broadcast_in_dim.72), channel_id=1, replica_groups=mesh['z'=4,'y'=2,'x'=4,'w'=2,'c'=2] {'z','y'}, dimensions={0} | all-to-all | bytes 3145728 | tf_op jit(solution)/shard_map/all_to_all | solution.py:43
  521.4 26.3 %reduce-scatter.8.cloned.1.call-done = bf16[512,256]{1,0:T(8,128)(2,1)} async-done(((bf16[4096,256]{1,0:T(8,128)(2,1)}), bf16[512,256]{1,0:T(8,128)(2,1)}) %reduce-scatter.8.cloned.1.call-update) | async-done | bytes 262160 | tf_op jit(solution)/shard_map/reduce_scatter | solution.py:340
  547.7 53.9 %reduce-scatter.6.cloned.1.call-done = bf16[512,256]{1,0:T(8,128)(2,1)} async-done(((bf16[4096,256]{1,0:T(8,128)(2,1)}), bf16[512,256]{1,0:T(8,128)(2,1)}) %reduce-scatter.6.cloned.1.call-update) | async-done | bytes 262160 | tf_op jit(solution)/shard_map/reduce_scatter | solution.py:340
  (239 shorter events, 103.9 us)
Async XLA Ops:
  7.2 11.5 %copy-start.28 = (bf16[2,256,512]{2,1,0:T(8,128)(2,1)S(1)}, bf16[2,256,512]{2,1,0:T(8,128)(2,1)}, u32[]{:S(2)}) copy-start(bf16[2,256,512]{2,1,0:T(8,128)(2,1)} %param.21) | copy-start | bytes 1572868
  11.2 23.1 %all-to-all-start = ((bf16[8,16,4096]{2,1,0:T(8,128)(2,1)}), bf16[8,16,4096]{2,1,0:T(8,128)(2,1)S(1)}, u32[]{:S(2)}, u32[]{:S(2)}) async-start(bf16[8,16,4096]{2,1,0:T(8,128)(2,1)} %broadcast_in_dim.28), calls=%async_computation | async-start | bytes 2097152 | tf_op jit(solution)/shard_map/all_to_all | solution.py:43
  18.7 109.9 %all-gather.4.cloned.1.call-start = ((), (), s32[]{:S(2)}) async-start(), calls=%async_computation.13 | async-start | bytes 2359296 | tf_op jit(solution)/shard_map/all_gather | solution.py:275
  34.3 75.4 %copy-start.4 = (bf16[8,16,4096]{2,1,0:T(8,128)(2,1)}, bf16[8,16,4096]{2,1,0:T(8,128)(2,1)S(1)}, u32[]{:S(2)}) copy-start(bf16[8,16,4096]{2,1,0:T(8,128)(2,1)S(1)} %all-to-all-done) | copy-start | bytes 3145732
  36.3 73.4 %all-to-all-start.2 = ((bf16[8,512,384]{2,1,0:T(8,128)(2,1)}), bf16[8,512,384]{2,1,0:T(8,128)(2,1)}, u32[]{:S(2)}, u32[]{:S(2)}) async-start(bf16[8,512,384]{2,1,0:T(8,128)(2,1)} %broadcast_in_dim.29), calls=%async_computation.2 | async-start | bytes 6291456 | tf_op jit(solution)/shard_map/all_to_all | solution.py:43
  46.1 5.5 collective-permute-start
  113.2 6.0 collective-permute-start.1
  130.9 4.6 collective-permute-start.2
  137.2 37.6 %all-to-all-start.3 = ((bf16[8,16,8192]{2,1,0:T(8,128)(2,1)}), bf16[8,16,8192]{2,1,0:T(8,128)(2,1)S(1)}, u32[]{:S(2)}, u32[]{:S(2)}) async-start(bf16[8,16,8192]{2,1,0:T(8,128)(2,1)} %bitcast.106), calls=%async_computation.3 | async-start | bytes 4194304 | tf_op jit(solution)/shard_map/all_to_all | solution.py:43
  143.4 104.7 %all-gather.6.cloned.1.call-start = ((), (), s32[]{:S(2)}) async-start(), calls=%async_computation.14 | async-start | bytes 3538944 | tf_op jit(solution)/shard_map/all_gather | solution.py:274
  143.6 31.4 %copy-start.10 = (bf16[16,4096]{1,0:T(8,128)(2,1)S(1)}, bf16[16,4096]{1,0:T(8,128)(2,1)}, u32[]{:S(2)}) copy-start(bf16[16,4096]{1,0:T(8,128)(2,1)} %param.11) | copy-start | bytes 393220
  144.7 159.0 %all-gather.8.cloned.1.call-start = ((), (), s32[]{:S(2)}) async-start(), calls=%async_computation.15 | async-start | bytes 2359296 | tf_op jit(solution)/shard_map/all_gather | solution.py:275
  176.0 38.7 %copy-start.6 = (bf16[4096,64]{0,1:T(8,128)(2,1)S(1)}, bf16[4096,64]{0,1:T(8,128)(2,1)}, u32[]{:S(2)}) copy-start(bf16[4096,64]{0,1:T(8,128)(2,1)} %get-tuple-element.63) | copy-start | bytes 1572868
  213.3 6.3 %collective-permute-start.3 = (bf16[128,8192]{1,0:T(8,128)(2,1)S(1)}, bf16[128,8192]{1,0:T(8,128)(2,1)}, u32[]{:S(2)}, u32[]{:S(2)}) collective-permute-start(bf16[128,8192]{1,0:T(8,128)(2,1)S(1)} %bitcast.104), channel_id=1, source_target_pairs={{0,1},{1,0},{2,3},{3,2},{4,5},{5,4},{6,7},{7,6},{8,9},{9,8},{10,11... | collective-permute-start | bytes 6291464 | tf_op jit(solution)/shard_map/ppermute | solution.py:39
  254.1 3.4 collective-permute-start.4
  262.6 41.0 %copy-start.34 = (bf16[256,256]{1,0:T(8,128)(2,1)S(1)}, bf16[256,256]{1,0:T(8,128)(2,1)}, u32[]{:S(2)}) copy-start(bf16[256,256]{1,0:T(8,128)(2,1)} %get-tuple-element.29) | copy-start | bytes 393220
  305.9 3.8 collective-permute-start.5
  311.4 21.9 %all-to-all-start.5 = ((bf16[8,16,4096]{2,1,0:T(8,128)(2,1)}), bf16[8,16,4096]{2,1,0:T(8,128)(2,1)S(1)}, u32[]{:S(2)}, u32[]{:S(2)}) async-start(bf16[8,16,4096]{2,1,0:T(8,128)(2,1)} %bitcast.28), calls=%async_computation.5 | async-start | bytes 2097152 | tf_op jit(solution)/shard_map/all_to_all | solution.py:43
  317.5 200.6 %reduce-scatter.4.cloned.1.call-start = ((), (), s32[]{:S(2)}) async-start(), calls=%async_computation.16 | async-start | bytes 3538944 | tf_op jit(solution)/shard_map/reduce_scatter | solution.py:356
  318.3 34.5 %copy-start.40 = (f32[16]{0:T(128)}, f32[16]{0:T(128)S(1)}, u32[]{:S(2)}) copy-start(f32[16]{0:T(128)S(1)} %compare_convert_fusion) | copy-start | bytes 196
  352.8 4.7 collective-permute-start.6
  366.3 1.5 collective-permute-start.7
  375.8 2.7 collective-permute-start.8
  380.8 22.1 %all-to-all-start.7 = ((bf16[8,16,4096]{2,1,0:T(8,128)(2,1)}), bf16[8,16,4096]{2,1,0:T(8,128)(2,1)S(1)}, u32[]{:S(2)}, u32[]{:S(2)}) async-start(bf16[8,16,4096]{2,1,0:T(8,128)(2,1)} %bitcast.116), calls=%async_computation.7 | async-start | bytes 2097152 | tf_op jit(solution)/shard_map/all_to_all | solution.py:43
  384.5 163.2 %reduce-scatter.8.cloned.1.call-start = ((), (), s32[]{:S(2)}) async-start(), calls=%async_computation.18 | async-start | bytes 2359296 | tf_op jit(solution)/shard_map/reduce_scatter | solution.py:340
  387.9 15.3 %copy-start.39 = (f32[16]{0:T(128)S(1)}, f32[16]{0:T(128)}, u32[]{:S(2)}) copy-start(f32[16]{0:T(128)} %copy-done.38) | copy-start | bytes 196
  387.9 15.3 %copy-start.41 = (f32[16]{0:T(128)S(1)}, f32[16]{0:T(128)}, u32[]{:S(2)}) copy-start(f32[16]{0:T(128)} %copy-done.40) | copy-start | bytes 196
  387.9 213.6 %reduce-scatter.6.cloned.1.call-start = ((), (), s32[]{:S(2)}) async-start(), calls=%async_computation.17 | async-start | bytes 2359296 | tf_op jit(solution)/shard_map/reduce_scatter | solution.py:340
  403.2 24.2 %copy-start.5 = (bf16[8,16,4096]{2,1,0:T(8,128)(2,1)S(1)}, bf16[8,16,4096]{2,1,0:T(8,128)(2,1)}, u32[]{:S(2)}) copy-start(bf16[8,16,4096]{2,1,0:T(8,128)(2,1)} %copy-done.4) | copy-start | bytes 3145732
  425.9 4.1 collective-permute-start.9
  435.3 48.4 %all-to-all-start.1 = ((bf16[8,256,512]{2,1,0:T(8,128)(2,1)}), bf16[8,256,512]{2,1,0:T(8,128)(2,1)S(1)}, u32[]{:S(2)}, u32[]{:S(2)}) async-start(bf16[8,256,512]{2,1,0:T(8,128)(2,1)} %maximum_bitcast_fusion), calls=%async_computation.1 | async-start | bytes 4194304 | tf_op jit(solution)/shard_map/all_to_all | solution.py:43
  446.6 1.4 collective-permute-start.10
  (36 other events, 135.0 us)
Sparse Core Ops, SparseCore 0:
  21.1 83.0 all-gather.3
  145.9 102.2 all-gather.5
  249.8 53.7 all-gather.7
  371.5 105.4 reduce-scatter.3
  479.2 68.4 reduce-scatter.7
  549.9 51.5 reduce-scatter.5

commit v2 on v1

--- a/solution.py
+++ b/solution.py
@@ -1,4 +1,3 @@
-import functools
 import math
 
 import jax
@@ -8,6 +7,7 @@
 from jax.experimental.pallas import tpu as pltpu
 from jax.sharding import Mesh
 from jax.sharding import PartitionSpec as P
+
 
 HD = 128
 LEN = 256
@@ -47,6 +47,47 @@
     return jnp.broadcast_to(value[None], (lax.axis_size(axis),) + value.shape)
 
 
+def beside(own, other, axis):
+    first = lax.axis_index(axis) == 0
+    return jnp.concatenate(
+        [jnp.where(first, own, other), jnp.where(first, other, own)], axis=0
+    )
+
+
+def swap(value, axis):
+    return lax.ppermute(value, axis, [(0, 1), (1, 0)])
+
+
+def ring_blocks(block, axis):
+    count = lax.axis_size(axis)
+    place = lax.axis_index(axis)
+    middle = block.shape[0] // 2
+    up = [(source, (source + 1) % count) for source in range(count)]
+    down = [(source, (source - 1) % count) for source in range(count)]
+    after = lax.ppermute(block, axis, down)
+    before = lax.ppermute(block, axis, up)
+    far_low = lax.ppermute(after[:middle], axis, down)
+    far_high = lax.ppermute(before[middle:], axis, up)
+    rows = block.shape[0]
+    starts = [((place + step) % count) * rows for step in (0, 1, 3, 2, 2)]
+    starts[4] = starts[4] + middle
+    return list(zip(starts, (block, after, before, far_low, far_high)))
+
+
+def block_matmul(left_side, blocks):
+    return sum(
+        matmul(lax.dynamic_slice_in_dim(left_side, start, block.shape[0], 1), block)
+        for start, block in blocks
+    )
+
+
+def own_and_other(both, axis):
+    first = lax.axis_index(axis) == 0
+    middle = both.shape[0] // 2
+    low, high = both[:middle], both[middle:]
+    return jnp.where(first, low, high), jnp.where(first, high, low)
+
+
 def gather_rows(share):
     mine = exchange(copies(share, CHIPS), CHIPS).reshape(-1, share.shape[-1])
     return (mine, core_swap(mine))
@@ -70,12 +111,9 @@
 def attend_kernel(
     size_ref,
     core_ref,
-    query_ref,
-    own_ref,
+    primal_ref,
+    moved_ref,
     other_ref,
-    tangent_query_ref,
-    tangent_own_ref,
-    tangent_other_ref,
     cosine_ref,
     sine_ref,
     row_ref,
@@ -91,28 +129,31 @@
     low_core = core_ref[0] == 0
     cosine = cosine_ref[...]
     sine = sine_ref[...]
-    lane = lax.broadcasted_iota(jnp.int32, own_ref.shape, 1)
+    count, width = queries_ref.shape
+    half = count // 2
+    lane = lax.broadcasted_iota(jnp.int32, (count, HD), 1)
     lower = lane < HD // 2
 
-    def join(own, other):
+    def join(own, at):
+        other = jnp.concatenate([other_ref[half:, at], other_ref[:half, at]], axis=0).astype(F32)
         first = jnp.where(low_core, own, other)
         second = jnp.where(low_core, other, own)
         key = jnp.where(lower, first, half_turn(second))
         value = jnp.where(lower, half_turn(first), second)
         return rope(key, cosine, sine, half_turn).astype(BF), value.astype(BF)
 
-    key, value = join(own_ref[...], other_ref[...].astype(F32))
-    tangent_key, tangent_value = join(tangent_own_ref[...], tangent_other_ref[...].astype(F32))
+    key, value = join(primal_ref[:, width:], slice(0, HD))
+    tangent_key, tangent_value = join(moved_ref[:, width:], slice(HD, 2 * HD))
     keys_ref[...] = key
     values_ref[...] = value
     rows = row_ref[...]
     columns = column_ref[...]
     allowed = (columns <= rows) & (columns < size)
     scaling = 1.0 / math.sqrt(HD)
-    for head in range(query_ref.shape[1] // HD):
+    for head in range(width // HD):
         at = slice(head * HD, (head + 1) * HD)
-        query = rope(query_ref[:, at], cosine, sine, half_turn).astype(BF)
-        tangent_query = rope(tangent_query_ref[:, at], cosine, sine, half_turn).astype(BF)
+        query = rope(primal_ref[:, at], cosine, sine, half_turn).astype(BF)
+        tangent_query = rope(moved_ref[:, at], cosine, sine, half_turn).astype(BF)
         scores = contract_last(query, key) * scaling
         powers = jnp.where(allowed, jnp.exp(scores), 0.0)
         weights = powers / jnp.sum(powers, axis=-1, keepdims=True)
@@ -130,8 +171,9 @@
         weights_ref[head] = weights
 
 
-def attend(size, core, query, own, other, tangent_query, tangent_own, tangent_other, tables):
-    rows, width = query.shape
+def attend(size, core, primal, moved, other, tables):
+    rows, width = primal.shape
+    width = width - HD
     wide = jax.ShapeDtypeStruct((rows, width), BF)
     narrow = jax.ShapeDtypeStruct((rows, HD), BF)
     weights = jax.ShapeDtypeStruct((width // HD, rows, rows), F32)
@@ -140,13 +182,14 @@
     return pl.pallas_call(
         attend_kernel,
         out_shape=(wide, wide, wide, narrow, narrow, weights),
-        in_specs=[smem] * 2 + [vmem] * 10,
+        in_specs=[smem] * 2 + [vmem] * 7,
         out_specs=(vmem,) * 6,
         name="attend",
-    )(size, core, query, own, other, tangent_query, tangent_own, tangent_other, *tables)
+    )(size, core, primal, moved, other, *tables)
 
 
 def attend_back_kernel(
+    core_ref,
     weights_ref,
     queries_ref,
     keys_ref,
@@ -155,9 +198,10 @@
     cosine_ref,
     sine_ref,
     grad_query_ref,
-    grad_key_ref,
-    grad_value_ref,
+    own_ref,
+    other_ref,
 ):
+    low_core = core_ref[0] == 0
     cosine = cosine_ref[...]
     sine = -sine_ref[...]
     key = keys_ref[...]
@@ -177,11 +221,16 @@
             matmul(grad_scores, key), cosine, sine, half_turn
         ).astype(BF)
         grad_key = grad_key + contract_rows(grad_scores, queries_ref[:, at])
-    grad_key_ref[...] = rope(grad_key, cosine, sine, half_turn).astype(BF)
-    grad_value_ref[...] = grad_value.astype(BF)
-
-
-def attend_back(weights, queries, keys, values, grad, cosine, sine):
+    grad_key = rope(grad_key, cosine, sine, half_turn)
+    lower = lax.broadcasted_iota(jnp.int32, grad_key.shape, 1) < HD // 2
+    low_part = jnp.where(lower, grad_key, half_turn(grad_value))
+    high_part = jnp.where(lower, half_turn(grad_key), grad_value)
+    own_ref[...] = jnp.where(low_core, low_part, high_part).astype(BF)
+    other_ref[...] = jnp.where(low_core, high_part, low_part).astype(BF)
+
+
+def attend_back(core, weights, queries, keys, values, grad, cosine, sine):
+    smem = pl.BlockSpec(memory_space=pltpu.SMEM)
     vmem = pl.BlockSpec(memory_space=pltpu.VMEM)
     return pl.pallas_call(
         attend_back_kernel,
@@ -190,10 +239,10 @@
             jax.ShapeDtypeStruct(keys.shape, BF),
             jax.ShapeDtypeStruct(values.shape, BF),
         ),
-        in_specs=[vmem] * 7,
+        in_specs=[smem] + [vmem] * 7,
         out_specs=(vmem,) * 3,
         name="attend_back",
-    )(weights, queries, keys, values, grad, cosine, sine)
+    )(core, weights, queries, keys, values, grad, cosine, sine)
 
 
 def normalize(stream, gain_row):
@@ -215,7 +264,7 @@
     return inverse * (scaled - wide_stream * inverse * inverse * shift)
 
 
-def body(
+def program(
     tokens,
     lengths,
     norm_gains,
@@ -234,7 +283,6 @@
     batches = lax.axis_size(DP)
     core = lax.axis_index("c")
     chip = lax.axis_index(CHIPS)
-    low_core = core == 0
     rows = LEN
     half = rows // 2
     size = lax.dynamic_slice_in_dim(lengths, lax.axis_index(DP), 1)
@@ -257,10 +305,10 @@
     def turned(values):
         return jnp.concatenate([values[half:], values[:half]], axis=0)
 
-    weights = [
-        jnp.concatenate([query_weight[n], key_weight[n], value_weight[n]], axis=1)
-        for n in range(layer_count)
-    ]
+    weights = []
+    for n in range(layer_count):
+        packed = jnp.concatenate([query_weight[n], key_weight[n], value_weight[n]], axis=1)
+        weights.append(lax.optimization_barrier(packed))
     probes = [
         jnp.concatenate([query_probe[n], key_probe[n], value_probe[n]], axis=1)
         for n in range(layer_count)
@@ -268,11 +316,20 @@
     out_turned = [out_probe[n].T for n in range(layer_count)]
     full_probes = [None] * layer_count
     full_out = [None] * layer_count
-    full_probes[0] = exchange(copies(probes[0], DP), DP).reshape(features, -1)
-    for n in range(layer_count):
-        if n > 0:
-            full_probes[n] = lax.all_gather(probes[n], DP, axis=0, tiled=True)
-        full_out[n] = lax.all_gather(out_turned[n], DP, axis=0, tiled=True)
+    arrived = swap(probes[0], "y")
+    pair = beside(probes[0], arrived, "y")
+    probe_blocks = ring_blocks(pair, "z")
+    arrived = swap(out_turned[0], "y")
+    pair = beside(out_turned[0], arrived, "y")
+    full_out[0] = lax.all_gather(pair, "z", axis=0, tiled=True)
+    for n in range(1, layer_count):
+        later = jnp.concatenate([probes[n], out_turned[n]], axis=1)
+        arrived = swap(later, "y")
+        later = beside(later, arrived, "y")
+        probe_pair = later[:, : probes[n].shape[1]]
+        out_pair = later[:, probes[n].shape[1] :]
+        full_probes[n] = lax.all_gather(probe_pair, "z", axis=0, tiled=True)
+        full_out[n] = lax.all_gather(out_pair, "z", axis=0, tiled=True)
 
     stream = tokens
     tangent = None
@@ -286,29 +343,37 @@
             normed_halves = gather_rows(normed)
             both = jnp.concatenate(normed_halves, axis=0)
             primal = matmul(both, weights[n])
-            moved = matmul(both, full_probes[n])
+            moved = block_matmul(both, probe_blocks)
         else:
             tangent_normed = norm_tangent(wide_stream, inverse, tangent, gain_row)
-            joined = gather_rows(jnp.concatenate([normed, tangent_normed], axis=1))
-            both = jnp.concatenate([part[:, :features] for part in joined], axis=0)
-            tangent_both = jnp.concatenate([part[:, features:] for part in joined], axis=0)
-            primal = matmul(both, weights[n])
-            moved = matmul(both, full_probes[n]) + matmul(tangent_both, weights[n])
+            joined = gather_rows(jnp.concatenate([normed, tangent_normed], axis=0))
+
+            def split(values):
+                return values.reshape(-1, 2, share_rows, values.shape[-1])
+
+            both = jnp.concatenate(
+                [split(part)[:, 0].reshape(half, features) for part in joined], axis=0
+            )
+            both = lax.optimization_barrier(both)
+            own_way = [split(matmul(part, weights[n])) for part in joined]
+            probe_way = [split(matmul(part, full_probes[n])) for part in joined]
+            primal = jnp.concatenate(
+                [part[:, 0].reshape(half, -1) for part in own_way], axis=0
+            )
+            moved = jnp.concatenate(
+                [
+                    (part[:, 1] + probed[:, 0]).reshape(half, -1)
+                    for part, probed in zip(own_way, probe_way)
+                ],
+                axis=0,
+            )
         if n == 0:
             pieces = jnp.moveaxis(both.reshape(rows, batches, -1), 1, 0)
             all_rows = exchange(pieces, DP).reshape(batches * rows, -1)
         own = jnp.concatenate([primal[:, query_width:], moved[:, query_width:]], axis=1)
-        other = turned(core_swap(own.astype(BF)))
+        other = core_swap(own.astype(BF))
         blended, tangent_blended, queries, keys, values, attention = attend(
-            size,
-            core_word,
-            primal[:, :query_width],
-            own[:, :HD],
-            other[:, :HD],
-            moved[:, :query_width],
-            own[:, HD:],
-            other[:, HD:],
-            tables,
+            size, core_word, primal, moved, other, tables
         )
 
         def out_terms(at):
@@ -337,29 +402,36 @@
         cotangent_both = jnp.concatenate(gather_rows(cotangent.astype(BF)), axis=0)
         grad_mixed = contract_last(cotangent_both, out_weight[n]).astype(BF)
         out_term = contract_rows(cotangent_both, blended).astype(BF)
-        out_products[n] = lax.psum_scatter(out_term, DP, scatter_dimension=0, tiled=True)
-        query_low, key_low, value_low = attend_back(
-            attention, queries, keys, values, grad_mixed, cosine, sine
+        partial = lax.psum_scatter(out_term, "z", scatter_dimension=0, tiled=True)
+        own_part, other_part = own_and_other(partial, "y")
+        arrived = swap(other_part, "y")
+        out_products[n] = own_part.astype(F32) + arrived.astype(F32)
+        query_low, own_part, other_part = attend_back(
+            core_word, attention, queries, keys, values, grad_mixed, cosine, sine
         )
-        key_value = jnp.concatenate([key_low, value_low], axis=1).reshape(rows, 2, 2, half_width)
-        own_part = jnp.where(low_core, key_value[:, :, 0], key_value[:, :, 1])
-        other_part = jnp.where(low_core, key_value[:, :, 1], key_value[:, :, 0])
-        arrived = turned(core_swap(other_part.reshape(rows, -1)))
-        pair = (own_part.reshape(rows, -1).astype(F32) + arrived.astype(F32)).astype(BF)
+        arrived = turned(core_swap(other_part))
+        pair = (own_part.astype(F32) + arrived.astype(F32)).astype(BF)
         grads = jnp.concatenate([query_low, pair], axis=1)
         if n > 0:
-            own_terms = contract_last(grads[:half], weights[n])
             other_terms = contract_last(grads[half:], weights[n])
+            own_terms = contract_last(grads[:half], lax.optimization_barrier(weights[n]))
             grad_normed = sum_rows(own_terms, other_terms)
             cotangent = cotangent + norm_back(wide_stream, inverse, grad_normed, norm_gains[n])
             term = contract_rows(both, grads).astype(BF)
-            projected[n] = lax.psum_scatter(term, DP, scatter_dimension=0, tiled=True).astype(F32)
+            partial = lax.psum_scatter(term, "z", scatter_dimension=0, tiled=True)
+            own_part, other_part = own_and_other(partial, "y")
+            arrived = swap(other_part, "y")
+            projected[n] = own_part.astype(F32) + arrived.astype(F32)
         else:
-            all_grads = exchange(copies(grads, DP), DP).reshape(batches * rows, -1)
-            projected[n] = contract_rows(all_rows, all_grads)
+            arrived = swap(grads, "y")
+            blocks = ring_blocks(beside(grads, arrived, "y"), "z")
+            projected[n] = sum(
+                contract_rows(lax.dynamic_slice_in_dim(all_rows, start, block.shape[0], 0), block)
+                for start, block in blocks
+            )
     projected = jnp.stack(projected)
     key_end = query_width + half_width
-    out_stack = jnp.stack([product.astype(F32).T for product in out_products])
+    out_stack = jnp.stack([product.T for product in out_products])
     return (
         projected[:, :, :query_width],
         projected[:, :, query_width:key_end],
@@ -385,7 +457,7 @@
         P(None, tensor, DP),
     )
     return jax.shard_map(
-        body,
+        program,
         mesh=inner,
         in_specs=placed,
         out_specs=(

time: 612 us -> 467 us (0.76)
  the two profiles are of different devices: /device:TPU:1 before, /device:TPU:8 now
where the time goes in v2:
time: 467 us; the launch traced here: 458 us
  waiting for transfers between devices  138 us (30%)
  blocking collectives  94.1 us (20%)
  matrix products  58.8 us (13%)
  local copies, waits for them, and re-layouts  48.1 us (10%)
  starting transfers between devices  46.7 us (10%)
  other arithmetic  42 us (9%)
  between operations  15.6 us (3%)
  Pallas kernels  14.6 us (3%)
    all_to_all x4, blocking collectives, exchange(): return lax.all_to_all(pieces, axis, split_axis=0, concat_axis=0, tiled=True)  94.1 us
    ppermute x7, waiting for transfers between devices, swap(): return lax.ppermute(value, axis, [(0, 1), (1, 0)])  65 us
    all_to_all x4, starting transfers between devices, exchange(): return lax.all_to_all(pieces, axis, split_axis=0, concat_axis=0, tiled=True)  24.1 us
    dot_general x15, matrix products, matmul(): return jnp.dot(left_side, right_side, preferred_element_type=F32)  23.4 us
    dot_general x8, matrix products, contract_last(): lax.dot_general(left_side, right_side, (((1,), (1,)), ((), ())), preferre...  17.7 us
    all_to_all x4, waiting for transfers between devices, exchange(): return lax.all_to_all(pieces, axis, split_axis=0, concat_axis=0, tiled=True)  16 us
    dot_general x8, matrix products, contract_rows(): lax.dot_general(left_side, right_side, (((0,), (0,)), ((), ())), preferre...  14.7 us
    ppermute x2, waiting for transfers between devices, ring_blocks(): far_high = lax.ppermute(before[middle:], axis, up)  13.9 us
  transfers between devices with their start and end apart: 36, of which 16 were waited for; matrix products, arithmetic and copies ran while one was open for 26% of the time, Pallas kernels for 3%

profile of v2, /device:TPU:8, one launch (start us, length us, event | category | flops | bytes accessed | tf_op | source)
XLA Modules:
  0.0 458.0 jit_solution(4447753200559381609)
XLA Ops:
  12.6 6.4 %all-to-all-start = ((bf16[8,16,4096]{2,1,0:T(8,128)(2,1)}), bf16[8,16,4096]{2,1,0:T(8,128)(2,1)S(1)}, u32[]{:S(2)}, u32[]{:S(2)}) async-start(bf16[8,16,4096]{2,1,0:T(8,128)(2,1)} %broadcast_in_dim.24), calls=%async_computation | async-start | bytes 2097152 | tf_op jit(solution)/shard_map/all_to_all | solution.py:43
  21.9 4.5 slice_bitcast_fusion
  43.6 4.2 pad_maximum_fusion.1
  47.8 9.1 %collective-permute-done.3 = bf16[1024,384]{0,1:T(8,128)(2,1)} collective-permute-done((bf16[1024,384]{0,1:T(8,128)(2,1)}, bf16[1024,384]{0,1:T(8,128)(2,1)}, u32[]{:S(2)}, u32[]{:S(2)}) %collective-permute-start.3) | collective-permute-done | bytes 786464 | tf_op jit(solution)/shard_map/ppermute | solution.py:68
  59.8 3.2 collective-permute-start.4
  64.9 13.9 %collective-permute-done.5 = bf16[512,384]{0,1:T(8,128)(2,1)S(1)} collective-permute-done((bf16[512,384]{0,1:T(8,128)(2,1)S(1)}, bf16[512,384]{0,1:T(8,128)(2,1)S(1)}, u32[]{:S(2)}, u32[]{:S(2)}) %collective-permute-start.5) | collective-permute-done | bytes 393248 | tf_op jit(solution)/shard_map/ppermute | solution.py:70
  92.0 4.4 attend.2
  108.1 6.7 %all-to-all-start.2 = ((bf16[8,16,8192]{2,1,0:T(8,128)(2,1)}), bf16[8,16,8192]{2,1,0:T(8,128)(2,1)}, u32[]{:S(2)}, u32[]{:S(2)}) async-start(bf16[8,16,8192]{2,1,0:T(8,128)(2,1)} %bitcast.152), calls=%async_computation.2 | async-start | bytes 4194304 | tf_op jit(solution)/shard_map/all_to_all | solution.py:43
  116.8 37.0 %collective-permute-done.10 = bf16[512,640]{1,0:T(8,128)(2,1)S(1)} collective-permute-done((bf16[512,640]{1,0:T(8,128)(2,1)S(1)}, bf16[512,640]{1,0:T(8,128)(2,1)S(1)}, u32[]{:S(2)}, u32[]{:S(2)}) %collective-permute-start.10) | collective-permute-done | bytes 655392 | tf_op jit(solution)/shard_map/ppermute | solution.py:58
  158.7 34.6 %all_to_all.40 = bf16[8,32,4096]{2,1,0:T(8,128)(2,1)} all-to-all(bf16[8,32,4096]{2,1,0:T(8,128)(2,1)S(1)} %broadcast_in_dim.56), channel_id=1, replica_groups=mesh['z'=4,'y'=2,'x'=4,'w'=2,'c'=2] {'x','w'}, dimensions={0} | all-to-all | bytes 4194304 | tf_op jit(solution)/shard_map/all_to_all | solution.py:43
  199.1 2.9 pad_maximum_fusion.2
  202.0 4.0 fusion.7
  206.9 3.1 fusion.37
  210.2 3.2 fusion.167
  219.3 4.4 attend.3
  223.6 7.9 %all-gather.8.cloned.1.call-done = bf16[4096,256]{1,0:T(8,128)(2,1)} async-done(((bf16[1024,256]{1,0:T(8,128)(2,1)}), bf16[4096,256]{1,0:T(8,128)(2,1)}) %all-gather.8.cloned.1.call-update) | async-done | bytes 2097168 | tf_op jit(solution)/shard_map/all_gather | solution.py:332
  240.2 5.8 %all-to-all-start.4 = ((bf16[8,16,4096]{2,1,0:T(8,128)(2,1)}), bf16[8,16,4096]{2,1,0:T(8,128)(2,1)}, u32[]{:S(2)}, u32[]{:S(2)}) async-start(bf16[8,16,4096]{2,1,0:T(8,128)(2,1)} %bitcast.153), calls=%async_computation.4 | async-start | bytes 2097152 | tf_op jit(solution)/shard_map/all_to_all | solution.py:43
  246.7 16.0 %all-to-all-done.4 = bf16[8,16,4096]{2,1,0:T(8,128)(2,1)} async-done(((bf16[8,16,4096]{2,1,0:T(8,128)(2,1)}), bf16[8,16,4096]{2,1,0:T(8,128)(2,1)}, u32[]{:S(2)}, u32[]{:S(2)}) %all-to-all-start.4) | async-done | bytes 1048608 | tf_op jit(solution)/shard_map/all_to_all | solution.py:43
  264.2 20.2 %all_to_all.41 = bf16[8,16,4096]{2,1,0:T(8,128)(2,1)S(1)} all-to-all(bf16[8,16,4096]{2,1,0:T(8,128)(2,1)S(1)} %broadcast_in_dim.57), channel_id=1, replica_groups=mesh['z'=4,'y'=2,'x'=4,'w'=2,'c'=2] {'x','w'}, dimensions={0} | all-to-all | bytes 2097152 | tf_op jit(solution)/shard_map/all_to_all | solution.py:43
  295.4 3.3 fusion.34.grad_ref
  298.6 2.9 attend_back.2
  306.4 3.2 convolution_convert_fusion.3
  313.5 20.1 %all_to_all.42 = bf16[8,16,4096]{2,1,0:T(8,128)(2,1)S(1)} all-to-all(bf16[8,16,4096]{2,1,0:T(8,128)(2,1)S(1)} %bitcast.158), channel_id=1, replica_groups=mesh['z'=4,'y'=2,'x'=4,'w'=2,'c'=2] {'x','w'}, dimensions={0} | all-to-all | bytes 2097152 | tf_op jit(solution)/shard_map/all_to_all | solution.py:43
  334.1 19.2 %all_to_all.43 = bf16[8,16,4096]{2,1,0:T(8,128)(2,1)S(1)} all-to-all(bf16[8,16,4096]{2,1,0:T(8,128)(2,1)S(1)} %broadcast_in_dim.58), channel_id=1, replica_groups=mesh['z'=4,'y'=2,'x'=4,'w'=2,'c'=2] {'x','w'}, dimensions={0} | all-to-all | bytes 2097152 | tf_op jit(solution)/shard_map/all_to_all | solution.py:43
  365.2 5.1 %all-to-all-start.1 = ((bf16[8,256,512]{2,1,0:T(8,128)(2,1)}), bf16[8,256,512]{2,1,0:T(8,128)(2,1)S(1)}, u32[]{:S(2)}, u32[]{:S(2)}) async-start(bf16[8,256,512]{2,1,0:T(8,128)(2,1)} %copy.87), calls=%async_computation.1 | async-start | bytes 4194304 | tf_op jit(solution)/shard_map/all_to_all | solution.py:43
  370.4 3.3 fusion.31.grad_ref
  373.7 2.9 attend_back.3
  383.8 15.5 %collective-permute-done.18 = bf16[256,384]{1,0:T(8,128)(2,1)} collective-permute-done((bf16[256,384]{1,0:T(8,128)(2,1)S(1)}, bf16[256,384]{1,0:T(8,128)(2,1)}, u32[]{:S(2)}, u32[]{:S(2)}) %collective-permute-start.18) | collective-permute-done | bytes 196640 | tf_op jit(solution)/shard_map/ppermute | solution.py:58
  401.2 3.0 collective-permute-start.19
  405.4 12.8 %collective-permute-done.19 = bf16[512,384]{1,0:T(8,128)(2,1)} collective-permute-done((bf16[512,384]{1,0:T(8,128)(2,1)}, bf16[512,384]{1,0:T(8,128)(2,1)}, u32[]{:S(2)}, u32[]{:S(2)}) %collective-permute-start.19) | collective-permute-done | bytes 393248 | tf_op jit(solution)/shard_map/ppermute | solution.py:67
  431.9 8.0 %collective-permute-done.23 = bf16[512,384]{0,1:T(8,128)(2,1)S(1)} collective-permute-done((bf16[512,384]{0,1:T(8,128)(2,1)S(1)}, bf16[512,384]{0,1:T(8,128)(2,1)S(1)}, u32[]{:S(2)}, u32[]{:S(2)}) %collective-permute-start.23) | collective-permute-done | bytes 393248 | tf_op jit(solution)/shard_map/ppermute | solution.py:58
  443.8 4.5 collective-permute-done.24
  (285 shorter events, 147.2 us)
Async XLA Ops:
  10.8 22.8 %collective-permute-start.1 = (bf16[512,384]{0,1:T(8,128)(2,1)S(1)}, bf16[512,384]{0,1:T(8,128)(2,1)}, u32[]{:S(2)}, u32[]{:S(2)}) collective-permute-start(bf16[512,384]{0,1:T(8,128)(2,1)S(1)} %pad_maximum_fusion.23), channel_id=1, source_target_pairs={{0,16},{16,0},{1,17},{17,1},{2,18},{18,2},{3,19},{19,3},{4,20},{20... | collective-permute-start | bytes 1179656 | tf_op jit(solution)/shard_map/ppermute | solution.py:58
  12.6 29.1 %all-to-all-start = ((bf16[8,16,4096]{2,1,0:T(8,128)(2,1)}), bf16[8,16,4096]{2,1,0:T(8,128)(2,1)S(1)}, u32[]{:S(2)}, u32[]{:S(2)}) async-start(bf16[8,16,4096]{2,1,0:T(8,128)(2,1)} %broadcast_in_dim.24), calls=%async_computation | async-start | bytes 2097152 | tf_op jit(solution)/shard_map/all_to_all | solution.py:43
  19.0 79.5 %all-gather.4.cloned.1.call-start = ((), (), s32[]{:S(2)}) async-start(), calls=%async_computation.11 | async-start | bytes 2621440 | tf_op jit(solution)/shard_map/all_gather | solution.py:324
  19.9 19.9 %collective-permute-start.7 = (bf16[512,256]{1,0:T(8,128)(2,1)S(1)}, bf16[512,256]{1,0:T(8,128)(2,1)}, u32[]{:S(2)}, u32[]{:S(2)}) collective-permute-start(bf16[512,256]{1,0:T(8,128)(2,1)S(1)} %bitcast.181), channel_id=1, source_target_pairs={{0,16},{16,0},{1,17},{17,1},{2,18},{18,2},{3,19},{19,3},{4,20},{20... | collective-permute-start | bytes 786440 | tf_op jit(solution)/shard_map/ppermute | solution.py:58
  35.8 21.1 %collective-permute-start.3 = (bf16[1024,384]{0,1:T(8,128)(2,1)}, bf16[1024,384]{0,1:T(8,128)(2,1)}, u32[]{:S(2)}, u32[]{:S(2)}) collective-permute-start(bf16[1024,384]{0,1:T(8,128)(2,1)} %pad_maximum_fusion.17), channel_id=1, source_target_pairs={{0,32},{32,64},{64,96},{96,0},{1,33},{33,65},{65,97},{97,1},{2,34}... | collective-permute-start | bytes 2359304 | tf_op jit(solution)/shard_map/ppermute | solution.py:68
  37.8 20.3 %collective-permute-start.2 = (bf16[1024,384]{0,1:T(8,128)(2,1)}, bf16[1024,384]{0,1:T(8,128)(2,1)}, u32[]{:S(2)}, u32[]{:S(2)}) collective-permute-start(bf16[1024,384]{0,1:T(8,128)(2,1)} %pad_maximum_fusion.17), channel_id=1, source_target_pairs={{0,96},{32,0},{64,32},{96,64},{1,97},{33,1},{65,33},{97,65},{2,98}... | collective-permute-start | bytes 2359304 | tf_op jit(solution)/shard_map/ppermute | solution.py:67
  41.7 37.1 %collective-permute-start = (bf16[128,4096]{1,0:T(8,128)(2,1)S(1)}, bf16[128,4096]{1,0:T(8,128)(2,1)S(1)}, u32[]{:S(2)}, u32[]{:S(2)}) collective-permute-start(bf16[128,4096]{1,0:T(8,128)(2,1)S(1)} %bitcast.139), channel_id=1, source_target_pairs={{0,1},{1,0},{2,3},{3,2},{4,5},{5,4},{6,7},{7,6},{8,9},{9,8},{10,11... | collective-permute-start | bytes 3145736 | tf_op jit(solution)/shard_map/ppermute | solution.py:39
  57.9 20.9 %collective-permute-start.5 = (bf16[512,384]{0,1:T(8,128)(2,1)S(1)}, bf16[512,384]{0,1:T(8,128)(2,1)S(1)}, u32[]{:S(2)}, u32[]{:S(2)}) collective-permute-start(bf16[512,384]{0,1:T(8,128)(2,1)S(1)} %slice.258), channel_id=1, source_target_pairs={{0,32},{32,64},{64,96},{96,0},{1,33},{33,65},{65,97},{97,1},{2,34}... | collective-permute-start | bytes 1179656 | tf_op jit(solution)/shard_map/ppermute | solution.py:70
  59.8 20.3 %collective-permute-start.4 = (bf16[512,384]{0,1:T(8,128)(2,1)}, bf16[512,384]{0,1:T(8,128)(2,1)}, u32[]{:S(2)}, u32[]{:S(2)}) collective-permute-start(bf16[512,384]{0,1:T(8,128)(2,1)} %slice.257), channel_id=1, source_target_pairs={{0,96},{32,0},{64,32},{96,64},{1,97},{33,1},{65,33},{97,65},{2,98}... | collective-permute-start | bytes 1179656 | tf_op jit(solution)/shard_map/ppermute | solution.py:69
  88.1 3.3 collective-permute-start.6
  102.0 4.4 collective-permute-start.8
  108.1 48.0 %all-to-all-start.2 = ((bf16[8,16,8192]{2,1,0:T(8,128)(2,1)}), bf16[8,16,8192]{2,1,0:T(8,128)(2,1)}, u32[]{:S(2)}, u32[]{:S(2)}) async-start(bf16[8,16,8192]{2,1,0:T(8,128)(2,1)} %bitcast.152), calls=%async_computation.2 | async-start | bytes 4194304 | tf_op jit(solution)/shard_map/all_to_all | solution.py:43
  114.9 92.0 %all-gather.6.cloned.1.call-start = ((), (), s32[]{:S(2)}) async-start(), calls=%async_computation.12 | async-start | bytes 3932160 | tf_op jit(solution)/shard_map/all_gather | solution.py:331
  115.5 38.2 %collective-permute-start.10 = (bf16[512,640]{1,0:T(8,128)(2,1)S(1)}, bf16[512,640]{1,0:T(8,128)(2,1)S(1)}, u32[]{:S(2)}, u32[]{:S(2)}) collective-permute-start(bf16[512,640]{1,0:T(8,128)(2,1)S(1)} %pad_maximum_fusion.18), channel_id=1, source_target_pairs={{0,16},{16,0},{1,17},{17,1},{2,18},{18,2},{3,19},{19,3},{4,20},{20... | collective-permute-start | bytes 1966088 | tf_op jit(solution)/shard_map/ppermute | solution.py:58
  156.1 75.5 %all-gather.8.cloned.1.call-start = ((), (), s32[]{:S(2)}) async-start(), calls=%async_computation.13 | async-start | bytes 2621440 | tf_op jit(solution)/shard_map/all_gather | solution.py:332
  193.3 16.6 %collective-permute-start.9 = (bf16[256,4096]{1,0:T(8,128)(2,1)}, bf16[256,4096]{1,0:T(8,128)(2,1)}, u32[]{:S(2)}, u32[]{:S(2)}) collective-permute-start(bf16[256,4096]{1,0:T(8,128)(2,1)} %bitcast.26), channel_id=1, source_target_pairs={{0,1},{1,0},{2,3},{3,2},{4,5},{5,4},{6,7},{7,6},{8,9},{9,8},{10,11... | collective-permute-start | bytes 6291464 | tf_op jit(solution)/shard_map/ppermute | solution.py:39
  235.9 2.7 collective-permute-start.12
  240.2 22.4 %all-to-all-start.4 = ((bf16[8,16,4096]{2,1,0:T(8,128)(2,1)}), bf16[8,16,4096]{2,1,0:T(8,128)(2,1)}, u32[]{:S(2)}, u32[]{:S(2)}) async-start(bf16[8,16,4096]{2,1,0:T(8,128)(2,1)} %bitcast.153), calls=%async_computation.4 | async-start | bytes 2097152 | tf_op jit(solution)/shard_map/all_to_all | solution.py:43
  246.0 134.0 %reduce-scatter.8.cloned.1.call-start = ((), (), s32[]{:S(2)}) async-start(), calls=%async_computation.16 | async-start | bytes 2621440 | tf_op jit(solution)/shard_map/reduce_scatter | solution.py:405
  284.5 2.7 collective-permute-start.13
  290.3 137.7 %reduce-scatter.4.cloned.1.call-start = ((), (), s32[]{:S(2)}) async-start(), calls=%async_computation.14 | async-start | bytes 3932160 | tf_op jit(solution)/shard_map/reduce_scatter | solution.py:421
  306.3 133.8 %reduce-scatter.6.cloned.1.call-start = ((), (), s32[]{:S(2)}) async-start(), calls=%async_computation.15 | async-start | bytes 2621440 | tf_op jit(solution)/shard_map/reduce_scatter | solution.py:405
  309.6 2.7 collective-permute-start.15
  365.2 57.0 %all-to-all-start.1 = ((bf16[8,256,512]{2,1,0:T(8,128)(2,1)}), bf16[8,256,512]{2,1,0:T(8,128)(2,1)S(1)}, u32[]{:S(2)}, u32[]{:S(2)}) async-start(bf16[8,256,512]{2,1,0:T(8,128)(2,1)} %copy.87), calls=%async_computation.1 | async-start | bytes 4194304 | tf_op jit(solution)/shard_map/all_to_all | solution.py:43
  379.9 19.5 %collective-permute-start.18 = (bf16[256,384]{1,0:T(8,128)(2,1)S(1)}, bf16[256,384]{1,0:T(8,128)(2,1)}, u32[]{:S(2)}, u32[]{:S(2)}) collective-permute-start(bf16[256,384]{1,0:T(8,128)(2,1)S(1)} %pad_maximum_fusion.29), channel_id=1, source_target_pairs={{0,16},{16,0},{1,17},{17,1},{2,18},{18,2},{3,19},{19,3},{4,20},{20... | collective-permute-start | bytes 589832 | tf_op jit(solution)/shard_map/ppermute | solution.py:58
  381.9 22.6 %collective-permute-start.25 = (bf16[512,256]{1,0:T(8,128)(2,1)}, bf16[512,256]{1,0:T(8,128)(2,1)S(1)}, u32[]{:S(2)}, u32[]{:S(2)}) collective-permute-start(bf16[512,256]{1,0:T(8,128)(2,1)} %broadcast_select_fusion.5), channel_id=1, source_target_pairs={{0,16},{16,0},{1,17},{17,1},{2,18},{18,2},{3,19},{19,3},{4,20},{20... | collective-permute-start | bytes 786440 | tf_op jit(solution)/shard_map/ppermute | solution.py:58
  401.2 16.9 %collective-permute-start.19 = (bf16[512,384]{1,0:T(8,128)(2,1)}, bf16[512,384]{1,0:T(8,128)(2,1)}, u32[]{:S(2)}, u32[]{:S(2)}) collective-permute-start(bf16[512,384]{1,0:T(8,128)(2,1)} %pad_maximum_fusion.24), channel_id=1, source_target_pairs={{0,96},{32,0},{64,32},{96,64},{1,97},{33,1},{65,33},{97,65},{2,98}... | collective-permute-start | bytes 1179656 | tf_op jit(solution)/shard_map/ppermute | solution.py:67
  404.2 16.7 %collective-permute-start.20 = (bf16[512,384]{1,0:T(8,128)(2,1)}, bf16[512,384]{1,0:T(8,128)(2,1)}, u32[]{:S(2)}, u32[]{:S(2)}) collective-permute-start(bf16[512,384]{1,0:T(8,128)(2,1)} %pad_maximum_fusion.24), channel_id=1, source_target_pairs={{0,32},{32,64},{64,96},{96,0},{1,33},{33,65},{65,97},{97,1},{2,34}... | collective-permute-start | bytes 1179656 | tf_op jit(solution)/shard_map/ppermute | solution.py:68
  419.1 7.7 %collective-permute-start.21 = (bf16[256,384]{1,0:T(8,128)(2,1)S(1)}, bf16[256,384]{1,0:T(8,128)(2,1)S(1)}, u32[]{:S(2)}, u32[]{:S(2)}) collective-permute-start(bf16[256,384]{1,0:T(8,128)(2,1)S(1)} %slice.282), channel_id=1, source_target_pairs={{0,96},{32,0},{64,32},{96,64},{1,97},{33,1},{65,33},{97,65},{2,98}... | collective-permute-start | bytes 589832 | tf_op jit(solution)/shard_map/ppermute | solution.py:69
  421.8 8.1 %collective-permute-start.22 = (bf16[256,384]{1,0:T(8,128)(2,1)S(1)}, bf16[256,384]{1,0:T(8,128)(2,1)S(1)}, u32[]{:S(2)}, u32[]{:S(2)}) collective-permute-start(bf16[256,384]{1,0:T(8,128)(2,1)S(1)} %slice.283), channel_id=1, source_target_pairs={{0,32},{32,64},{64,96},{96,0},{1,33},{33,65},{65,97},{97,1},{2,34}... | collective-permute-start | bytes 589832 | tf_op jit(solution)/shard_map/ppermute | solution.py:70
  429.3 10.7 %collective-permute-start.23 = (bf16[512,384]{0,1:T(8,128)(2,1)S(1)}, bf16[512,384]{0,1:T(8,128)(2,1)S(1)}, u32[]{:S(2)}, u32[]{:S(2)}) collective-permute-start(bf16[512,384]{0,1:T(8,128)(2,1)S(1)} %broadcast_select_fusion.2), channel_id=1, source_target_pairs={{0,16},{16,0},{1,17},{17,1},{2,18},{18,2},{3,19},{19,3},{4,20},{20... | collective-permute-start | bytes 1179656 | tf_op jit(solution)/shard_map/ppermute | solution.py:58
  441.2 7.1 %collective-permute-start.24 = (bf16[512,256]{1,0:T(8,128)(2,1)S(1)}, bf16[512,256]{1,0:T(8,128)(2,1)}, u32[]{:S(2)}, u32[]{:S(2)}) collective-permute-start(bf16[512,256]{1,0:T(8,128)(2,1)S(1)} %broadcast_select_fusion.6), channel_id=1, source_target_pairs={{0,16},{16,0},{1,17},{17,1},{2,18},{18,2},{3,19},{19,3},{4,20},{20... | collective-permute-start | bytes 786440 | tf_op jit(solution)/shard_map/ppermute | solution.py:58
  (55 other events, 328.7 us)
Sparse Core Ops, SparseCore 0:
  43.7 40.6 all-gather.3
  156.2 42.5 all-gather.5
  200.5 31.0 all-gather.7
  290.4 27.0 reduce-scatter.7
  319.8 38.0 reduce-scatter.3
  360.1 55.0 reduce-scatter.5
